TPU v7x, 16 devices: a whole 2x2x2 slice. The times are simulated.
16 devices in a mesh: stage: 2 (over z), expert: 8 (over y, x, core).
Axes of the slice: x: 2, y: 2, z: 2, core: 2. Of those that a mesh axis runs over, the one named last changes fastest.
Arguments:
- tokens_in: bfloat16 [2, 2048, 768], P('stage', 'expert')
- expert_ids: int32 [2, 2048, 1], P('stage', 'expert')
- gate_wts: float32 [2, 2048, 1], P('stage', 'expert')
- w_gate: bfloat16 [2, 8, 768, 3072], P('stage', 'expert')
- w_up: bfloat16 [2, 8, 768, 3072], P('stage', 'expert')
- w_down: bfloat16 [2, 8, 3072, 768], P('stage', 'expert')
- grad_out: bfloat16 [2, 2048, 768], P('stage', 'expert')
Outputs:
- output 1: bfloat16 [2, 2048, 768], P('stage', 'expert')
- output 2: bfloat16 [2, 2048, 768], P('stage', 'expert')
- output 3: bfloat16 [2, 8, 768, 3072], P('stage', 'expert')
- output 4: bfloat16 [2, 8, 768, 3072], P('stage', 'expert')
- output 5: bfloat16 [2, 8, 3072, 768], P('stage', 'expert')
All inputs are finite; a program needn't handle non-finite values.
Results may differ from a plain program's by a relative error of at most 0.001.
Values are sent between devices in bfloat16 or wider.
A program may use at most 1 GiB of HBM per device.

v0:
```python
import jax
import jax.numpy as jnp
from jax import lax
from jax.sharding import PartitionSpec as P


def slot_table(rel_ids, n_local, capacity):
    is_held = (rel_ids >= 0) & (rel_ids < n_local)
    one_hot = (rel_ids[:, None] == jnp.arange(n_local, dtype=jnp.int32)[None, :]).astype(jnp.int32)
    slot_rank = jnp.sum((jnp.cumsum(one_hot, axis=0) - 1) * one_hot, axis=1)
    return jnp.where(is_held, rel_ids * capacity + slot_rank, n_local * capacity)


def row_table(slot_idx, capacity_rows):
    asg_count = slot_idx.shape[0]
    return jnp.full((capacity_rows,), asg_count, jnp.int32).at[slot_idx].set(jnp.arange(asg_count, dtype=jnp.int32), mode="drop")


def solution(mesh):
    n_stage = mesh.shape["stage"]
    n_group = mesh.shape["expert"]
    half_stage = n_stage // 2
    send_to_b = [(src_row, src_row + half_stage) for src_row in range(half_stage)]
    send_to_a = [(src_row + half_stage, src_row) for src_row in range(half_stage)]
    tok_spec = P("stage", "expert", None)
    w_spec = P("stage", "expert", None, None)

    def device_fn(tokens_in, expert_ids, gate_wts, w_gate, w_up, w_down, grad_out):
        tok_count, d_model = tokens_in.shape[1], tokens_in.shape[2]
        top_k = expert_ids.shape[2]
        local_count = w_gate.shape[1]
        n_experts = local_count * n_group
        capacity = 3 * tok_count * top_k // (2 * n_experts)
        buf_shape = (n_group, local_count, capacity, d_model)
        tokens = lax.ppermute(tokens_in[0], "stage", send_to_b)
        route_ids = lax.ppermute(expert_ids[0], "stage", send_to_b)
        gate_vals = lax.ppermute(gate_wts[0], "stage", send_to_b)
        asg_row = row_table(slot_table(route_ids.reshape(-1), n_experts, capacity), n_experts * capacity)
        tok_row = asg_row // top_k
        gate_row = jnp.concatenate([gate_vals.reshape(-1), jnp.zeros((1,), jnp.float32)])[asg_row]
        tok_pad = jnp.concatenate([tokens, jnp.zeros((1, d_model), tokens.dtype)], axis=0)
        recv_x = lax.all_to_all(tok_pad[tok_row].reshape(buf_shape), "expert", 0, 0, tiled=True)
        w_gate_loc = w_gate[0]
        w_up_loc = w_up[0]
        w_down_loc = w_down[0]
        pre_gate = jnp.einsum("secd,edf->secf", recv_x, w_gate_loc, preferred_element_type=jnp.float32)
        pre_up = jnp.einsum("secd,edf->secf", recv_x, w_up_loc, preferred_element_type=jnp.float32)
        sig_gate = jax.nn.sigmoid(pre_gate)
        act_gate = pre_gate * sig_gate
        hidden = (act_gate * pre_up).astype(jnp.bfloat16)
        out_rows = jnp.einsum("secf,efd->secd", hidden, w_down_loc, preferred_element_type=jnp.float32).astype(jnp.bfloat16)
        back_y = lax.all_to_all(out_rows, "expert", 0, 0, tiled=True).reshape(-1, d_model)
        y_sum = jax.ops.segment_sum(gate_row[:, None] * back_y.astype(jnp.float32), tok_row, num_segments=tok_count + 1)
        y_local = y_sum[:tok_count].astype(jnp.bfloat16)
        dy_pad = jnp.concatenate([grad_out[0], jnp.zeros((1, d_model), grad_out.dtype)], axis=0)
        send_g = (gate_row[:, None] * dy_pad[tok_row].astype(jnp.float32)).astype(jnp.bfloat16).reshape(buf_shape)
        recv_g = lax.all_to_all(send_g, "expert", 0, 0, tiled=True)
        d_hidden = jnp.einsum("secd,efd->secf", recv_g, w_down_loc, preferred_element_type=jnp.float32)
        d_gate = (d_hidden * pre_up * sig_gate * (1.0 + pre_gate * (1.0 - sig_gate))).astype(jnp.bfloat16)
        d_up = (d_hidden * act_gate).astype(jnp.bfloat16)
        dx_rows = (jnp.einsum("secf,edf->secd", d_gate, w_gate_loc, preferred_element_type=jnp.float32) + jnp.einsum("secf,edf->secd", d_up, w_up_loc, preferred_element_type=jnp.float32)).astype(jnp.bfloat16)
        back_dx = lax.all_to_all(dx_rows, "expert", 0, 0, tiled=True).reshape(-1, d_model)
        dx_sum = jax.ops.segment_sum(back_dx.astype(jnp.float32), tok_row, num_segments=tok_count + 1)
        dx_local = lax.ppermute(dx_sum[:tok_count].astype(jnp.bfloat16), "stage", send_to_a)
        grad_wg = jnp.einsum("secd,secf->edf", recv_x, d_gate, preferred_element_type=jnp.float32).astype(jnp.bfloat16)
        grad_wu = jnp.einsum("secd,secf->edf", recv_x, d_up, preferred_element_type=jnp.float32).astype(jnp.bfloat16)
        grad_wd = jnp.einsum("secf,secd->efd", hidden, recv_g, preferred_element_type=jnp.float32).astype(jnp.bfloat16)
        return y_local[None], dx_local[None], grad_wg[None], grad_wu[None], grad_wd[None]

    return jax.shard_map(device_fn, mesh=mesh, in_specs=(tok_spec, tok_spec, tok_spec, w_spec, w_spec, w_spec, tok_spec), out_specs=(tok_spec, tok_spec, w_spec, w_spec, w_spec), check_vma=False)
```

profile of v0, /device:TPU:0, one launch (start us, length us, event | category | flops | bytes accessed | tf_op | source)
XLA Modules:
  0.0 106.0 jit_solution(3479433549976201444)
XLA Ops:
  0.6 5.2 %collective-permute-start = (s32[256,1]{0,1:T(1,128)}, s32[256,1]{0,1:T(1,128)S(1)}, u32[]{:S(2)}, u32[]{:S(2)}) collective-permute-start(s32[256,1]{0,1:T(1,128)} %bitcast.204), channel_id=1, source_target_pairs={{0,8},{1,9},{2,10},{3,11},{4,12},{5,13},{6,14},{7,15}} | collective-permute-start | bytes 3080 | tf_op jit(solution)/shard_map/ppermute | solution.py:36
  5.9 1.3 %collective-permute-start.1 = (f32[256,1]{0,1:T(1,128)}, f32[256,1]{0,1:T(1,128)S(1)}, u32[]{:S(2)}, u32[]{:S(2)}) collective-permute-start(f32[256,1]{0,1:T(1,128)} %bitcast.205), channel_id=1, source_target_pairs={{0,8},{1,9},{2,10},{3,11},{4,12},{5,13},{6,14},{7,15}} | collective-permute-start | bytes 3080 | tf_op jit(solution)/shard_map/ppermute | solution.py:37
  7.2 1.0 concatenate.11
  8.2 0.6 reduce-window.6
  8.8 0.2 slice_reduce_fusion
  9.2 1.4 %scatter_custom_fusion = s32[384]{0:T(512)S(1)} fusion(s32[256]{0:T(256)S(1)} %bitcast.198, s32[256]{0:T(256)S(1)} %iota.11, s32[]{:T(128)} %constant.13.clone.1), kind=kCustom, calls=%fused_computation.77 | custom fusion | bytes 1540 | tf_op jit(solution)/shard_map/scatter | solution.py:16
  10.6 2.8 %gather_fusion = f32[384]{0:T(512)S(1)} fusion(f32[257]{0:T(512)S(1)} %pad_maximum_fusion, s32[1024]{0:T(1024)S(1)} %pad_clamp_fusion), kind=kCustom, calls=%fused_computation | custom fusion | bytes 4608 | tf_op jit(solution)/shard_map/gather | solution.py:40
  13.5 2.2 %gather_fusion.2 = bf16[384,768]{1,0:T(8,128)(2,1)S(1)} fusion(bf16[257,768]{1,0:T(8,128)(2,1)S(1)} %concatenate.11, s32[1024]{0:T(1024)S(1)} %pad_clamp_fusion), kind=kCustom, calls=%fused_computation.2 | custom fusion | bytes 1181184 | tf_op jit(solution)/shard_map/gather | solution.py:56
  15.7 1.0 fusion.51
  16.7 3.7 %all-to-all-start.2 = ((bf16[8,1,48,768]{3,2,1,0:T(8,128)(2,1)}), bf16[8,1,48,768]{3,2,1,0:T(8,128)(2,1)S(1)}, u32[]{:S(2)}, u32[]{:S(2)}) async-start(bf16[8,1,48,768]{3,2,1,0:T(8,128)(2,1)} %fusion.51), calls=%async_computation.2 | async-start | bytes 1179648 | tf_op jit(solution)/shard_map/all_to_all | solution.py:57
  20.4 3.1 %collective-permute-start.2 = (bf16[256,768]{1,0:T(8,128)(2,1)S(1)}, bf16[256,768]{1,0:T(8,128)(2,1)S(1)}, u32[]{:S(2)}, u32[]{:S(2)}) collective-permute-start(bf16[256,768]{1,0:T(8,128)(2,1)S(1)} %bitcast.203), channel_id=1, source_target_pairs={{0,8},{1,9},{2,10},{3,11},{4,12},{5,13},{6,14},{7,15}} | collective-permute-start | bytes 1179656 | tf_op jit(solution)/shard_map/ppermute | solution.py:35
  23.5 9.0 %collective-permute-done.2 = bf16[256,768]{1,0:T(8,128)(2,1)S(1)} collective-permute-done((bf16[256,768]{1,0:T(8,128)(2,1)S(1)}, bf16[256,768]{1,0:T(8,128)(2,1)S(1)}, u32[]{:S(2)}, u32[]{:S(2)}) %collective-permute-start.2) | collective-permute-done | bytes 393248 | tf_op jit(solution)/shard_map/ppermute | solution.py:35
  32.5 2.6 %gather_fusion.1 = bf16[384,768]{1,0:T(8,128)(2,1)} fusion(bf16[257,768]{1,0:T(8,128)(2,1)S(1)} %concatenate.10, s32[1024]{0:T(1024)S(1)} %pad_clamp_fusion), kind=kCustom, calls=%fused_computation.1 | custom fusion | bytes 1181184 | tf_op jit(solution)/shard_map/gather | solution.py:42
  35.2 3.8 %all-to-all-start = ((bf16[8,1,48,768]{3,2,1,0:T(8,128)(2,1)}), bf16[8,1,48,768]{3,2,1,0:T(8,128)(2,1)S(1)}, u32[]{:S(2)}, u32[]{:S(2)}) async-start(bf16[8,1,48,768]{3,2,1,0:T(8,128)(2,1)} %bitcast.11), calls=%async_computation | async-start | bytes 1179648 | tf_op jit(solution)/shard_map/all_to_all | solution.py:42
  39.0 6.5 %fusion.13 = f32[8,48,3072]{2,1,0:T(8,128)} fusion(bf16[1,1,3072,768]{3,2,1,0:T(8,128)(2,1)} %param.12, bf16[8,1,48,768]{3,2,1,0:T(8,128)(2,1)S(1)} %all-to-all-done.2), kind=kOutput, calls=%fused_computation.25 | convolution fusion | flops 1811939328 | bytes 10027008 | tf_op jit(solution)/shard_map/secd,efd->secf/dot_general | solution.py:58
  45.5 3.9 %all-to-all-done = bf16[8,1,48,768]{3,2,1,0:T(8,128)(2,1)S(1)} async-done(((bf16[8,1,48,768]{3,2,1,0:T(8,128)(2,1)}), bf16[8,1,48,768]{3,2,1,0:T(8,128)(2,1)S(1)}, u32[]{:S(2)}, u32[]{:S(2)}) %all-to-all-start) | async-done | bytes 589856 | tf_op jit(solution)/shard_map/all_to_all | solution.py:42
  49.4 4.6 %fusion.10 = f32[8,48,3072]{2,1,0:T(8,128)S(1)} fusion(bf16[1,1,768,3072]{3,2,1,0:T(8,128)(2,1)} %param.10, bf16[8,1,48,768]{3,2,1,0:T(8,128)(2,1)S(1)} %all-to-all-done), kind=kOutput, calls=%fused_computation.21 | convolution fusion | flops 1811939328 | bytes 10027008 | tf_op jit(solution)/shard_map/secd,edf->secf/dot_general | solution.py:46
  54.0 8.4 %fusion.6 = (bf16[8,1,48,3072]{3,2,0,1:T(8,128)(2,1)S(1)}, bf16[8,48,3072]{2,1,0:T(8,128)(2,1)}, bf16[8,48,3072]{2,1,0:T(8,128)(2,1)S(1)}) fusion(f32[8,48,3072]{2,1,0:T(8,128)} %fusion.13, f32[8,48,3072]{2,1,0:T(8,128)S(1)} %fusion.10, bf16[1,1,768,3072]{3,2,1,0:T(8,128)(2,1)} %param.11, bf16[8,1,48,768]{3,2,1,0:T(8,128)(2,1)S(1)} %all-to-all-done), kind=kOutput, calls=%fused_computation.17 | convolution fusion | flops 1829634048 | bytes 21823488 | tf_op jit(solution)/shard_map/secd,edf->secf/dot_general | solution.py:47
  62.4 2.0 %fusion = f32[8,48,768]{2,1,0:T(8,128)S(1)} fusion(bf16[8,48,3072]{2,1,0:T(8,128)(2,1)S(1)} %get-tuple-element.7, bf16[1,1,768,3072]{3,2,1,0:T(8,128)(2,1)S(1)} %bitcast.200), kind=kOutput, calls=%fused_computation.9 | convolution fusion | flops 1811939328 | bytes 8257536 | tf_op jit(solution)/shard_map/secf,edf->secd/dot_general | solution.py:61
  64.5 2.9 %fusion.44 = bf16[8,1,48,768]{3,2,1,0:T(8,128)(2,1)} fusion(f32[8,48,768]{2,1,0:T(8,128)S(1)} %fusion, bf16[1,1,768,3072]{3,2,1,0:T(8,128)(2,1)S(1)} %bitcast.188, bf16[8,1,48,3072]{3,2,0,1:T(8,128)(2,1)S(1)} %get-tuple-element.5), kind=kOutput, calls=%fused_computation.47 | convolution fusion | flops 1812529152 | bytes 8847360 | tf_op jit(solution)/shard_map/secf,edf->secd/dot_general | solution.py:61
  67.4 3.8 %all-to-all-start.3 = ((bf16[8,1,48,768]{3,2,1,0:T(8,128)(2,1)}), bf16[8,1,48,768]{3,2,1,0:T(8,128)(2,1)S(1)}, u32[]{:S(2)}, u32[]{:S(2)}) async-start(bf16[8,1,48,768]{3,2,1,0:T(8,128)(2,1)} %fusion.44), calls=%async_computation.3 | async-start | bytes 1179648 | tf_op jit(solution)/shard_map/all_to_all | solution.py:62
  71.2 6.1 %fusion.21 = bf16[1,1,768,3072]{3,2,1,0:T(8,128)(2,1)} fusion(bf16[8,1,48,3072]{3,2,0,1:T(8,128)(2,1)} %copy-done.1, bf16[8,1,48,768]{3,2,1,0:T(8,128)(2,1)S(1)} %all-to-all-done), kind=kOutput, calls=%fused_computation.36 | convolution fusion | flops 1814298624 | bytes 7667712 | tf_op jit(solution)/shard_map/secd,secf->edf/dot_general | solution.py:65
  77.3 4.3 %fusion.23 = bf16[1,1,3072,768]{3,2,1,0:T(8,128)(2,1)} fusion(bf16[8,48,3072]{2,1,0:T(8,128)(2,1)S(1)} %copy-done.3, bf16[8,1,48,768]{3,2,1,0:T(8,128)(2,1)S(1)} %all-to-all-done.2), kind=kOutput, calls=%fused_computation.38 | convolution fusion | flops 1814298624 | bytes 7667712 | tf_op jit(solution)/shard_map/secf,secd->efd/dot_general | solution.py:67
  81.6 2.8 %fusion.41 = bf16[8,1,48,768]{3,2,1,0:T(8,128)(2,1)} fusion(bf16[8,48,3072]{2,1,0:T(8,128)(2,1)S(1)} %copy-done.3, bf16[1,1,3072,768]{3,2,1,0:T(8,128)(2,1)S(1)} %bitcast.202), kind=kOutput, calls=%fused_computation.46 | convolution fusion | flops 1812234240 | bytes 7667712 | tf_op jit(solution)/shard_map/secf,efd->secd/dot_general | solution.py:51
  84.4 3.9 %all-to-all-start.1 = ((bf16[8,1,48,768]{3,2,1,0:T(8,128)(2,1)}), bf16[8,1,48,768]{3,2,1,0:T(8,128)(2,1)S(1)}, u32[]{:S(2)}, u32[]{:S(2)}) async-start(bf16[8,1,48,768]{3,2,1,0:T(8,128)(2,1)} %fusion.41), calls=%async_computation.1 | async-start | bytes 1179648 | tf_op jit(solution)/shard_map/all_to_all | solution.py:52
  88.3 3.4 %scatter_custom_fusion.2 = f32[257,768]{1,0:T(8,128)S(1)} fusion(s32[384]{0:T(512)S(1)} %scatter_custom_fusion, bf16[384,768]{1,0:T(8,128)(2,1)S(1)} %bitcast.190, f32[]{:T(128)} %constant.12.clone.1), kind=kCustom, calls=%fused_computation.48 | custom fusion | flops 589824 | bytes 1379332 | tf_op jit(solution)/shard_map/scatter-add | solution.py:63
  91.8 1.3 %collective-permute-start.3 = (bf16[256,768]{1,0:T(8,128)(2,1)S(1)}, bf16[256,768]{1,0:T(8,128)(2,1)S(1)}, u32[]{:S(2)}, u32[]{:S(2)}) collective-permute-start(bf16[256,768]{1,0:T(8,128)(2,1)S(1)} %slice.32), channel_id=1, source_target_pairs={{8,0},{9,1},{10,2},{11,3},{12,4},{13,5},{14,6},{15,7}} | collective-permute-start | bytes 1179656 | tf_op jit(solution)/shard_map/ppermute | solution.py:64
  93.1 6.0 %fusion.22 = bf16[1,1,768,3072]{3,2,1,0:T(8,128)(2,1)} fusion(bf16[8,48,3072]{2,1,0:T(8,128)(2,1)} %copy-done.2, bf16[8,1,48,768]{3,2,1,0:T(8,128)(2,1)S(1)} %all-to-all-done), kind=kOutput, calls=%fused_computation.37 | convolution fusion | flops 1814298624 | bytes 7667712 | tf_op jit(solution)/shard_map/secd,secf->edf/dot_general | solution.py:66
  99.0 3.5 %scatter_custom_fusion.1 = f32[257,768]{1,0:T(8,128)S(1)} fusion(s32[384]{0:T(512)S(1)} %scatter_custom_fusion, bf16[384,768]{1,0:T(8,128)(2,1)S(1)} %bitcast.191, f32[384]{0:T(512)S(1)} %gather_fusion, f32[]{:T(128)} %constant.12.clone.1), kind=kCustom, calls=%fused_computation.53 | custom fusion | flops 884736 | bytes 1381380 | tf_op jit(solution)/shard_map/scatter-add | solution.py:53
  102.5 0.8 fusion.62
  103.3 2.0 %collective-permute-done.3 = bf16[256,768]{1,0:T(8,128)(2,1)S(1)} collective-permute-done((bf16[256,768]{1,0:T(8,128)(2,1)S(1)}, bf16[256,768]{1,0:T(8,128)(2,1)S(1)}, u32[]{:S(2)}, u32[]{:S(2)}) %collective-permute-start.3) | collective-permute-done | bytes 393248 | tf_op jit(solution)/shard_map/ppermute | solution.py:64
  105.3 0.7 copy.17
  (40 shorter events, 0.5 us)
Async XLA Ops:
  0.6 7.6 %collective-permute-start = (s32[256,1]{0,1:T(1,128)}, s32[256,1]{0,1:T(1,128)S(1)}, u32[]{:S(2)}, u32[]{:S(2)}) collective-permute-start(s32[256,1]{0,1:T(1,128)} %bitcast.204), channel_id=1, source_target_pairs={{0,8},{1,9},{2,10},{3,11},{4,12},{5,13},{6,14},{7,15}} | collective-permute-start | bytes 3080 | tf_op jit(solution)/shard_map/ppermute | solution.py:36
  5.9 4.7 %collective-permute-start.1 = (f32[256,1]{0,1:T(1,128)}, f32[256,1]{0,1:T(1,128)S(1)}, u32[]{:S(2)}, u32[]{:S(2)}) collective-permute-start(f32[256,1]{0,1:T(1,128)} %bitcast.205), channel_id=1, source_target_pairs={{0,8},{1,9},{2,10},{3,11},{4,12},{5,13},{6,14},{7,15}} | collective-permute-start | bytes 3080 | tf_op jit(solution)/shard_map/ppermute | solution.py:37
  10.6 9.8 %copy-start = (bf16[1,256,768]{2,1,0:T(8,128)(2,1)S(1)}, bf16[1,256,768]{2,1,0:T(8,128)(2,1)}, u32[]{:S(2)}) copy-start(bf16[1,256,768]{2,1,0:T(8,128)(2,1)} %param.7) | copy-start | bytes 1179652
  16.7 18.5 %all-to-all-start.2 = ((bf16[8,1,48,768]{3,2,1,0:T(8,128)(2,1)}), bf16[8,1,48,768]{3,2,1,0:T(8,128)(2,1)S(1)}, u32[]{:S(2)}, u32[]{:S(2)}) async-start(bf16[8,1,48,768]{3,2,1,0:T(8,128)(2,1)} %fusion.51), calls=%async_computation.2 | async-start | bytes 1179648 | tf_op jit(solution)/shard_map/all_to_all | solution.py:57
  20.4 12.1 %collective-permute-start.2 = (bf16[256,768]{1,0:T(8,128)(2,1)S(1)}, bf16[256,768]{1,0:T(8,128)(2,1)S(1)}, u32[]{:S(2)}, u32[]{:S(2)}) collective-permute-start(bf16[256,768]{1,0:T(8,128)(2,1)S(1)} %bitcast.203), channel_id=1, source_target_pairs={{0,8},{1,9},{2,10},{3,11},{4,12},{5,13},{6,14},{7,15}} | collective-permute-start | bytes 1179656 | tf_op jit(solution)/shard_map/ppermute | solution.py:35
  35.2 14.2 %all-to-all-start = ((bf16[8,1,48,768]{3,2,1,0:T(8,128)(2,1)}), bf16[8,1,48,768]{3,2,1,0:T(8,128)(2,1)S(1)}, u32[]{:S(2)}, u32[]{:S(2)}) async-start(bf16[8,1,48,768]{3,2,1,0:T(8,128)(2,1)} %bitcast.11), calls=%async_computation | async-start | bytes 1179648 | tf_op jit(solution)/shard_map/all_to_all | solution.py:42
  49.4 13.0 %slice-start.2 = ((s8[4718592]{0:T(1024)(128)(4,1)}), s8[4194304]{0:T(1024)(128)(4,1)S(1)}, s32[]{:S(2)}) async-start(s8[4718592]{0:T(1024)(128)(4,1)} %bitcast.199), calls=%async_computation.6 | async-start | bytes 8388608
  49.4 15.1 %slice-start = ((s8[4718592]{0:T(1024)(128)(4,1)}), s8[4194304]{0:T(1024)(128)(4,1)S(1)}, s32[]{:S(2)}) async-start(s8[4718592]{0:T(1024)(128)(4,1)} %bitcast.187), calls=%async_computation.4 | async-start | bytes 8388608
  54.0 8.4 %slice-start.3 = ((s8[4718592]{0:T(1024)(128)(4,1)}), s8[524288]{0:T(1024)(128)(4,1)S(1)}, s32[]{:S(2)}) async-start(s8[4718592]{0:T(1024)(128)(4,1)} %bitcast.199), calls=%async_computation.7 | async-start | bytes 1048576
  54.0 10.6 %slice-start.1 = ((s8[4718592]{0:T(1024)(128)(4,1)}), s8[524288]{0:T(1024)(128)(4,1)S(1)}, s32[]{:S(2)}) async-start(s8[4718592]{0:T(1024)(128)(4,1)} %bitcast.187), calls=%async_computation.5 | async-start | bytes 1048576
  62.4 2.1 %copy-start.2 = (bf16[8,48,3072]{2,1,0:T(8,128)(2,1)}, bf16[8,48,3072]{2,1,0:T(8,128)(2,1)S(1)}, u32[]{:S(2)}) copy-start(bf16[8,48,3072]{2,1,0:T(8,128)(2,1)S(1)} %get-tuple-element.7) | copy-start | bytes 7077892
  62.4 2.2 %copy-start.1 = (bf16[8,1,48,3072]{3,2,0,1:T(8,128)(2,1)}, bf16[8,1,48,3072]{3,2,0,1:T(8,128)(2,1)S(1)}, u32[]{:S(2)}) copy-start(bf16[8,1,48,3072]{3,2,0,1:T(8,128)(2,1)S(1)} %get-tuple-element.5) | copy-start | bytes 7077892
  67.4 17.0 %all-to-all-start.3 = ((bf16[8,1,48,768]{3,2,1,0:T(8,128)(2,1)}), bf16[8,1,48,768]{3,2,1,0:T(8,128)(2,1)S(1)}, u32[]{:S(2)}, u32[]{:S(2)}) async-start(bf16[8,1,48,768]{3,2,1,0:T(8,128)(2,1)} %fusion.44), calls=%async_computation.3 | async-start | bytes 1179648 | tf_op jit(solution)/shard_map/all_to_all | solution.py:62
  71.2 6.1 %copy-start.3 = (bf16[8,48,3072]{2,1,0:T(8,128)(2,1)S(1)}, bf16[8,48,3072]{2,1,0:T(8,128)(2,1)}, u32[]{:S(2)}) copy-start(bf16[8,48,3072]{2,1,0:T(8,128)(2,1)} %get-tuple-element.6) | copy-start | bytes 7077892
  71.2 10.4 %slice-start.4 = ((s8[4718592]{0:T(1024)(128)(4,1)}), s8[4194304]{0:T(1024)(128)(4,1)S(1)}, s32[]{:S(2)}) async-start(s8[4718592]{0:T(1024)(128)(4,1)} %bitcast.201), calls=%async_computation.8 | async-start | bytes 8388608
  77.3 4.3 %slice-start.5 = ((s8[4718592]{0:T(1024)(128)(4,1)}), s8[524288]{0:T(1024)(128)(4,1)S(1)}, s32[]{:S(2)}) async-start(s8[4718592]{0:T(1024)(128)(4,1)} %bitcast.201), calls=%async_computation.9 | async-start | bytes 1048576
  84.4 14.6 %all-to-all-start.1 = ((bf16[8,1,48,768]{3,2,1,0:T(8,128)(2,1)}), bf16[8,1,48,768]{3,2,1,0:T(8,128)(2,1)S(1)}, u32[]{:S(2)}, u32[]{:S(2)}) async-start(bf16[8,1,48,768]{3,2,1,0:T(8,128)(2,1)} %fusion.41), calls=%async_computation.1 | async-start | bytes 1179648 | tf_op jit(solution)/shard_map/all_to_all | solution.py:52
  91.8 13.5 %collective-permute-start.3 = (bf16[256,768]{1,0:T(8,128)(2,1)S(1)}, bf16[256,768]{1,0:T(8,128)(2,1)S(1)}, u32[]{:S(2)}, u32[]{:S(2)}) collective-permute-start(bf16[256,768]{1,0:T(8,128)(2,1)S(1)} %slice.32), channel_id=1, source_target_pairs={{8,0},{9,1},{10,2},{11,3},{12,4},{13,5},{14,6},{15,7}} | collective-permute-start | bytes 1179656 | tf_op jit(solution)/shard_map/ppermute | solution.py:64
where the time goes:
time: 107 us; the launch traced here: 106 us
  matrix products  43.5 us (41%)
  starting transfers between devices  26.1 us (24%)
  waiting for transfers between devices  14.8 us (14%)
  local copies, waits for them, and re-layouts  12.1 us (11%)
  other arithmetic  8.58 us (8%)
    ppermute x1, waiting for transfers between devices, device_fn(): tokens = lax.ppermute(tokens_in[0], 'stage', send_to_b)  8.97 us
    dot_general x1, matrix products, device_fn(): jnp.einsum('secd,edf->secf', recv_x, w_up_loc, preferred_element_type=jnp...  8.37 us
    dot_general x1, matrix products, device_fn(): jnp.einsum('secd,efd->secf', recv_g, w_down_loc, preferred_element_type=j...  6.54 us
    dot_general x1, matrix products, device_fn(): jnp.einsum('secd,secf->edf', recv_x, d_gate, preferred_element_type=jnp.f...  6.11 us
    dot_general x1, matrix products, device_fn(): jnp.einsum('secd,secf->edf', recv_x, d_up, preferred_element_type=jnp.flo...  5.95 us
    ppermute x1, starting transfers between devices, device_fn(): route_ids = lax.ppermute(expert_ids[0], 'stage', send_to_b)  5.22 us
    dot_general x1, matrix products, device_fn(): jnp.einsum('secd,edf->secf', recv_x, w_gate_loc, preferred_element_type=j...  4.55 us
    dot_general x1, matrix products, device_fn(): jnp.einsum('secf,secd->efd', hidden, recv_g, preferred_element_type=jnp.f...  4.28 us
  transfers between devices with their start and end apart: 8, of which 3 were waited for; matrix products, arithmetic and copies ran while one was open for 37% of the time, Pallas kernels for 0%

commit v1 on v0

v1 whole, which is shorter than its diff:
```python
import functools

import jax
import jax.numpy as jnp
from jax import lax
from jax.experimental import pallas as pl
from jax.experimental.pallas import tpu as pltpu
from jax.sharding import PartitionSpec as P

MESH = pl.DeviceIdType.MESH
BF16 = jnp.bfloat16
F32 = jnp.float32
COL = 256
TILE = 256
NT = (((1,), (1,)), ((), ()))
TN = (((0,), (0,)), ((), ()))


def dot(lhs, rhs, dims=(((1,), (0,)), ((), ()))):
    return lax.dot_general(lhs, rhs, dims, preferred_element_type=F32)


def slot_matrix(ids_row, n_exp, cap):
    n_tok = ids_row.shape[1]
    held = lax.broadcasted_iota(jnp.int32, (n_exp, n_tok), 0) == ids_row
    earlier = lax.broadcasted_iota(jnp.int32, (n_tok, n_tok), 0) < lax.broadcasted_iota(jnp.int32, (n_tok, n_tok), 1)
    counts = dot(held.astype(BF16), earlier.astype(BF16))
    rank = jnp.sum(jnp.where(held, counts, 0.0), axis=0, keepdims=True)
    slot = ids_row * cap + rank.astype(jnp.int32)
    return (lax.broadcasted_iota(jnp.int32, (n_exp * cap, n_tok), 0) == slot).astype(BF16)


def gate_column(gate_row):
    n_tok = gate_row.shape[1]
    eye = lax.broadcasted_iota(jnp.int32, (n_tok, n_tok), 0) == lax.broadcasted_iota(jnp.int32, (n_tok, n_tok), 1)
    return jnp.sum(jnp.where(eye, gate_row, 0.0), axis=1, keepdims=True)


def exchange_kernel(
    n_group, cap,
    ids_ref, gate_ref, x_ref, dy_ref, w1_hbm, w3_hbm, w2_hbm,
    y_ref, dx_ref, xr, qr, h_ref, da_ref, db_ref,
    w1, w3, w2, a_acc, b_acc, dh_acc, perm, xs, qs, dxs, dxr, os, yr, ids_m, gate_m,
    w_sem, meta_sem, xsend, xrecv, qsend, qrecv, dxsend, dxrecv, osend, yrecv,
):
    stage = lax.axis_index("stage")
    me = lax.axis_index("expert")
    n_chunk = xs.shape[0]
    n_rows = n_group * cap
    d_ff = w1.shape[1]
    n_tile = d_ff // TILE
    on_a = stage == 0
    on_b = stage == 1

    def block(index):
        return pl.ds(pl.multiple_of(index * cap, 16), cap)

    def send(src, dst, send_sem, recv_sem, to_stage, to):
        pltpu.make_async_remote_copy(
            src_ref=src, dst_ref=dst, send_sem=send_sem, recv_sem=recv_sem,
            device_id=(to_stage, to), device_id_type=MESH,
        ).start()

    def wait_recv(ref, sem):
        pltpu.make_async_copy(ref, ref, sem).wait()

    barrier = pltpu.get_barrier_semaphore()
    for other in range(1, 2 * n_group):
        flat = lax.rem(stage * n_group + me + other, 2 * n_group)
        pl.semaphore_signal(
            barrier, inc=1, device_id=(flat // n_group, lax.rem(flat, n_group)), device_id_type=MESH
        )

    w2_copy = pltpu.make_async_copy(w2_hbm, w2, w_sem.at[0])
    w1_copies = []
    w3_copies = []
    for c in range(n_chunk):
        rows = pl.ds(c * COL, COL)
        w1_copies.append(pltpu.make_async_copy(w1_hbm.at[rows], w1.at[rows], w_sem.at[1 + 2 * c]))
        w3_copies.append(pltpu.make_async_copy(w3_hbm.at[rows], w3.at[rows], w_sem.at[2 + 2 * c]))

    @pl.when(on_b)
    def _():
        w2_copy.start()
        for c in range(n_chunk):
            w1_copies[c].start()
            w3_copies[c].start()

    @pl.when(on_a)
    def _():
        perm[...] = slot_matrix(ids_ref[...], n_group, cap)
        xs[0] = dot(perm[...], x_ref[:, :COL]).astype(BF16)

    pl.semaphore_wait(barrier, 2 * n_group - 1)

    @pl.when(on_a)
    def _():
        send(ids_ref, ids_m, meta_sem.at[0], meta_sem.at[2], 1, me)
        send(gate_ref, gate_m, meta_sem.at[1], meta_sem.at[3], 1, me)
        for c in range(n_chunk):
            if c > 0:
                xs[c] = dot(perm[...], x_ref[:, c * COL:(c + 1) * COL]).astype(BF16)
            for k in range(n_group):
                to = lax.rem(me + k, n_group)
                send(xs.at[c, block(to)], xr.at[c, block(me)], xsend, xrecv.at[c], 1, to)
        y_ref[...] = jnp.zeros_like(y_ref)
        for c in range(n_chunk):
            wait_recv(dxr.at[c], dxrecv.at[c])
            dx_ref[:, c * COL:(c + 1) * COL] = dot(perm[...], dxr[c], TN).astype(BF16)
        wait_recv(ids_ref, meta_sem.at[0])
        wait_recv(gate_ref, meta_sem.at[1])
        wait_recv(xs, xsend)

    @pl.when(on_b)
    def _():
        wait_recv(ids_m, meta_sem.at[2])
        wait_recv(gate_m, meta_sem.at[3])
        perm[...] = slot_matrix(ids_m[...], n_group, cap)
        gate_col = gate_column(gate_m[...])
        gated = (gate_col * dy_ref[...].astype(F32)).astype(BF16)
        qs[...] = dot(perm[...], gated).astype(BF16)
        for k in range(1, n_group):
            to = lax.rem(me + k, n_group)
            send(qs.at[block(to)], qr.at[block(me)], qsend, qrecv, 1, to)
        qr[block(me), :] = qs[block(me), :]
        dx_ref[...] = jnp.zeros_like(dx_ref)
        w2_copy.wait()
        others = pl.ds(0, n_rows - cap)
        wait_recv(qr.at[others], qrecv)

        @pl.loop(0, n_tile)
        def _(j):
            cols = pl.ds(pl.multiple_of(j * TILE, TILE), TILE)
            dh_acc[:, cols] = dot(qr[...], w2[cols, :], NT)

        for c in range(n_chunk):
            w1_copies[c].wait()
            w3_copies[c].wait()
            wait_recv(xr.at[c], xrecv.at[c])
            rows = slice(c * COL, (c + 1) * COL)

            @pl.loop(0, n_tile)
            def _(j):
                cols = pl.ds(pl.multiple_of(j * TILE, TILE), TILE)
                a = dot(xr[c], w1[rows, cols])
                b = dot(xr[c], w3[rows, cols])
                if c > 0:
                    a = a + a_acc[:, cols]
                    b = b + b_acc[:, cols]
                if c < n_chunk - 1:
                    a_acc[:, cols] = a
                    b_acc[:, cols] = b
                else:
                    dh = dh_acc[:, cols]
                    sig = jax.nn.sigmoid(a)
                    act = a * sig
                    h_ref[:, cols] = (act * b).astype(BF16)
                    da_ref[:, cols] = (dh * b * sig * (1.0 + a * (1.0 - sig))).astype(BF16)
                    db_ref[:, cols] = (dh * act).astype(BF16)

        for c in range(n_chunk):
            rows = slice(c * COL, (c + 1) * COL)
            dxs[c] = (dot(da_ref[...], w1[rows, :], NT) + dot(db_ref[...], w3[rows, :], NT)).astype(BF16)
            for k in range(n_group):
                to = lax.rem(me + k, n_group)
                send(dxs.at[c, block(to)], dxr.at[c, block(me)], dxsend, dxrecv.at[c], 0, to)
        for c in range(n_chunk):
            os[c] = dot(h_ref[...], w2[:, c * COL:(c + 1) * COL]).astype(BF16)
            for k in range(1, n_group):
                to = lax.rem(me + k, n_group)
                send(os.at[c, block(to)], yr.at[c, block(me)], osend, yrecv.at[c], 1, to)
            yr[c, block(me), :] = os[c, block(me), :]
        for c in range(n_chunk):
            wait_recv(yr.at[c, others], yrecv.at[c])
            y_ref[:, c * COL:(c + 1) * COL] = (gate_col * dot(perm[...], yr[c], TN)).astype(BF16)
        wait_recv(qs.at[others], qsend)
        wait_recv(dxs, dxsend)
        wait_recv(os.at[:, others], osend)


def weight_grad_kernel(xr, qr, h_ref, da_ref, db_ref, y_in, dx_in, dw1, dw3, dw2, y_ref, dx_ref):
    step = pl.program_id(0)
    stage = lax.axis_index("stage")
    n_chunk = xr.shape[0]
    cols = pl.ds(pl.multiple_of(step * TILE, TILE), TILE)

    @pl.when(step == 0)
    def _():
        y_ref[...] = y_in[...]
        dx_ref[...] = dx_in[...]

    @pl.when(stage == 1)
    def _():
        for c in range(n_chunk):
            rows = slice(c * COL, (c + 1) * COL)
            dw1[rows, :] = dot(xr[c], da_ref[:, cols], TN).astype(BF16)
            dw3[rows, :] = dot(xr[c], db_ref[:, cols], TN).astype(BF16)
        dw2[...] = dot(h_ref[:, cols], qr[...], TN).astype(BF16)

    @pl.when(stage == 0)
    def _():
        dw1[...] = jnp.zeros_like(dw1)
        dw3[...] = jnp.zeros_like(dw3)
        dw2[...] = jnp.zeros_like(dw2)


def solution(mesh):
    n_group = mesh.shape["expert"]
    tok_spec = P("stage", "expert", None)
    w_spec = P("stage", "expert", None, None)

    def device_fn(tokens_in, expert_ids, gate_wts, w_gate, w_up, w_down, grad_out):
        n_tok, d_model = tokens_in.shape[1:]
        d_ff = w_gate.shape[3]
        cap = 3 * n_tok // (2 * n_group)
        n_rows = n_group * cap
        n_chunk = d_model // COL
        vmem = pl.BlockSpec(memory_space=pltpu.VMEM)
        hbm = pl.BlockSpec(memory_space=pl.ANY)
        chunked = (n_chunk, n_rows, COL)
        dma = pltpu.SemaphoreType.DMA
        y, dx, xr, qr, h, da, db = pl.pallas_call(
            functools.partial(exchange_kernel, n_group, cap),
            out_shape=(
                pltpu.VMEM((n_tok, d_model), BF16),
                pltpu.VMEM((n_tok, d_model), BF16),
                pltpu.VMEM(chunked, BF16),
                pltpu.VMEM((n_rows, d_model), BF16),
                pltpu.VMEM((n_rows, d_ff), BF16),
                pltpu.VMEM((n_rows, d_ff), BF16),
                pltpu.VMEM((n_rows, d_ff), BF16),
            ),
            in_specs=[vmem] * 4 + [hbm] * 3,
            out_specs=(vmem,) * 7,
            scratch_shapes=[
                pltpu.VMEM((d_model, d_ff), BF16),
                pltpu.VMEM((d_model, d_ff), BF16),
                pltpu.VMEM((d_ff, d_model), BF16),
                pltpu.VMEM((n_rows, d_ff), F32),
                pltpu.VMEM((n_rows, d_ff), F32),
                pltpu.VMEM((n_rows, d_ff), F32),
                pltpu.VMEM((n_rows, n_tok), BF16),
                pltpu.VMEM(chunked, BF16),
                pltpu.VMEM((n_rows, d_model), BF16),
                pltpu.VMEM(chunked, BF16),
                pltpu.VMEM(chunked, BF16),
                pltpu.VMEM(chunked, BF16),
                pltpu.VMEM(chunked, BF16),
                pltpu.VMEM((1, n_tok), jnp.int32),
                pltpu.VMEM((1, n_tok), F32),
                dma((1 + 2 * n_chunk,)),
                dma((4,)),
                dma(()),
                dma((n_chunk,)),
                dma(()),
                dma(()),
                dma(()),
                dma((n_chunk,)),
                dma(()),
                dma((n_chunk,)),
            ],
            compiler_params=pltpu.CompilerParams(
                collective_id=0, has_side_effects=True, vmem_limit_bytes=48 * 2**20
            ),
            name="exchange",
        )(
            expert_ids.reshape(1, n_tok), gate_wts.reshape(1, n_tok), tokens_in[0], grad_out[0],
            w_gate[0, 0], w_up[0, 0], w_down[0, 0],
        )
        held = [pltpu.with_memory_space_constraint(v, pltpu.VMEM) for v in (xr, qr, h, da, db, y, dx)]
        whole = pl.BlockSpec((n_tok, d_model), lambda j: (0, 0))
        dw1, dw3, dw2, y, dx = pl.pallas_call(
            weight_grad_kernel,
            grid=(d_ff // TILE,),
            out_shape=(
                jax.ShapeDtypeStruct((d_model, d_ff), BF16),
                jax.ShapeDtypeStruct((d_model, d_ff), BF16),
                jax.ShapeDtypeStruct((d_ff, d_model), BF16),
                jax.ShapeDtypeStruct((n_tok, d_model), BF16),
                jax.ShapeDtypeStruct((n_tok, d_model), BF16),
            ),
            in_specs=[vmem] * 7,
            out_specs=(
                pl.BlockSpec((d_model, TILE), lambda j: (0, j)),
                pl.BlockSpec((d_model, TILE), lambda j: (0, j)),
                pl.BlockSpec((TILE, d_model), lambda j: (j, 0)),
                whole,
                whole,
            ),
            compiler_params=pltpu.CompilerParams(vmem_limit_bytes=24 * 2**20),
            name="weight_grad",
        )(*held)
        return y[None], dx[None], dw1[None, None], dw3[None, None], dw2[None, None]

    return jax.shard_map(
        device_fn,
        mesh=mesh,
        in_specs=(tok_spec, tok_spec, tok_spec, w_spec, w_spec, w_spec, tok_spec),
        out_specs=(tok_spec, tok_spec, w_spec, w_spec, w_spec),
        check_vma=False,
    )
```

time: 107 us -> 63.9 us (0.60)
  the two profiles are of different devices: /device:TPU:0 before, /device:TPU:9 now
where the time goes in v1:
time: 63.9 us; the launch traced here: 63.7 us
  Pallas kernels  63 us (99%)
  between operations  0.64 us (1%)
    pallas_call x1, Pallas kernels, device_fn(): pl.pallas_call(functools.partial(exchange_kernel, n_group, cap), out_shap...  50.9 us
    pallas_call x1, Pallas kernels, device_fn(): pl.pallas_call(weight_grad_kernel, grid=(d_ff // TILE,), out_shape=(jax.S...  12.1 us

profile of v1, /device:TPU:9, one launch (start us, length us, event | category | flops | bytes accessed | tf_op | source)
XLA Modules:
  0.0 63.7 jit_solution(14758546577621125469)
XLA Ops:
  0.6 50.9 %exchange.1 = (bf16[256,768]{1,0:T(8,128)(2,1)S(1)}, bf16[256,768]{1,0:T(8,128)(2,1)S(1)}, bf16[3,384,256]{2,1,0:T(8,128)(2,1)S(1)}, bf16[384,768]{1,0:T(8,128)(...) custom-call(s32[1,256]{1,0:T(1,128)} %bitcast.17, ...), custom_call_target="tpu_custom_call" | custom-call | tf_op jit(solution)/shard_map/exchange/pallas_call | solution.py:222
  51.6 12.1 %weight_grad.1 = (bf16[768,3072]{1,0:T(8,128)(2,1)}, bf16[768,3072]{1,0:T(8,128)(2,1)}, bf16[3072,768]{1,0:T(8,128)(2,1)}, bf16[256,768]{1,0:T(8,128)(2,1)}, bf16[256,768]{1,0:T(8,128)(2,1)}) custom-call(bf16[3,384,256]{2,1,0:T(8,128)(2,1)S(1)} %get-tuple-element.17.xr, bf16[384,768]{1,0:T(8,128)(2,1)S(1)} %get-tuple-element.18.qr, ...), custom_call_target="tpu_custom_call" | custom-call | tf_op jit(solution)/shard_map/weight_grad/pallas_call | solution.py:272

commit v2 on v1

v2 whole, which is shorter than its diff:
```python
import functools

import jax
import jax.numpy as jnp
from jax import lax
from jax.experimental import pallas as pl
from jax.experimental.pallas import tpu as pltpu
from jax.sharding import PartitionSpec as P

MESH = pl.DeviceIdType.MESH
BF16 = jnp.bfloat16
F32 = jnp.float32
COL = 256
TILE = 256
N_CHUNK = 2
NT = (((1,), (1,)), ((), ()))
TN = (((0,), (0,)), ((), ()))
PEERS = ((0, 0, 0), (0, 0, 1), (1, 1, 0), (1, 1, 1), (0, 1, 0), (0, 1, 1), (1, 0, 0), (1, 0, 1))


def dot(lhs, rhs, dims=(((1,), (0,)), ((), ()))):
    return lax.dot_general(lhs, rhs, dims, preferred_element_type=F32)


def peer(me, place):
    y, x, core = PEERS[place]
    flip_y = lax.rem(me // 4 + y, 2)
    flip_x = lax.rem(lax.rem(me // 2, 2) + x, 2)
    return flip_y * 4 + flip_x * 2 + lax.rem(lax.rem(me, 2) + core, 2)


def slot_matrix(ids_row, n_exp, cap):
    n_tok = ids_row.shape[1]
    held = lax.broadcasted_iota(jnp.int32, (n_exp, n_tok), 0) == ids_row
    earlier = lax.broadcasted_iota(jnp.int32, (n_tok, n_tok), 0) < lax.broadcasted_iota(jnp.int32, (n_tok, n_tok), 1)
    counts = dot(held.astype(BF16), earlier.astype(BF16))
    rank = jnp.sum(jnp.where(held, counts, 0.0), axis=0, keepdims=True)
    slot = ids_row * cap + rank.astype(jnp.int32)
    return (lax.broadcasted_iota(jnp.int32, (n_exp * cap, n_tok), 0) == slot).astype(BF16)


def gate_column(gate_row):
    n_tok = gate_row.shape[1]
    eye = lax.broadcasted_iota(jnp.int32, (n_tok, n_tok), 0) == lax.broadcasted_iota(jnp.int32, (n_tok, n_tok), 1)
    return jnp.sum(jnp.where(eye, gate_row, 0.0), axis=1, keepdims=True)


def exchange_kernel(
    n_group, cap,
    ids_ref, gate_ref, x_ref, dy_ref, w1_hbm, w3_hbm, w2_hbm,
    y_ref, dx_ref, xt, db_ref, dw1, dw2,
    w1, w3, w2, xr, qr, h_ref, da_ref, perm, xs, qs, dxs, dxr, os, yr, ids_m, gate_m,
    w_sem, meta_sem, xsend, xrecv, qsend, qrecv, dxsend, dxrecv, osend, yrecv,
):
    stage = lax.axis_index("stage")
    me = lax.axis_index("expert")
    n_rows = n_group * cap
    d_model, d_ff = w1.shape
    n_col = d_model // COL
    per = n_group // N_CHUNK
    on_a = stage == 0
    on_b = stage == 1

    def block(index):
        return pl.ds(pl.multiple_of(index * cap, 16), cap)

    def place(k):
        return pl.ds(k * cap, cap)

    def send(src, dst, send_sem, recv_sem, to_stage, to):
        pltpu.make_async_remote_copy(
            src_ref=src, dst_ref=dst, send_sem=send_sem, recv_sem=recv_sem,
            device_id=(to_stage, to), device_id_type=MESH,
        ).start()

    def wait_bytes(ref, sem):
        pltpu.make_async_copy(ref, ref, sem).wait()

    barrier = pltpu.get_barrier_semaphore()
    for other in range(1, 2 * n_group):
        flat = lax.rem(stage * n_group + me + other, 2 * n_group)
        pl.semaphore_signal(
            barrier, inc=1, device_id=(flat // n_group, lax.rem(flat, n_group)), device_id_type=MESH
        )
    loads = [pltpu.make_async_copy(src, dst, w_sem.at[i]) for i, (src, dst) in enumerate(((w2_hbm, w2), (w1_hbm, w1), (w3_hbm, w3)))]

    @pl.when(on_b)
    def _():
        for load in loads:
            load.start()

    @pl.when(on_a)
    def _():
        perm[...] = slot_matrix(ids_ref[...], n_group, cap)
        xs[...] = dot(perm[...], x_ref[...]).astype(BF16)

    pl.semaphore_wait(barrier, 2 * n_group - 1)

    @pl.when(on_a)
    def _():
        send(ids_ref, ids_m, meta_sem.at[0], meta_sem.at[2], 1, me)
        send(gate_ref, gate_m, meta_sem.at[1], meta_sem.at[3], 1, me)
        for k in range(n_group):
            to = peer(me, k)
            send(xs.at[block(to)], xr.at[place(k)], xsend, xrecv.at[k // per], 1, to)
        y_ref[...] = jnp.zeros_like(y_ref)
        dw1[...] = jnp.zeros_like(dw1)
        dw2[...] = jnp.zeros_like(dw2)
        for c in range(n_col):
            wait_bytes(dxr.at[c], dxrecv.at[c])
            dx_ref[:, c * COL:(c + 1) * COL] = dot(perm[...], dxr[c], TN).astype(BF16)
        wait_bytes(ids_ref, meta_sem.at[0])
        wait_bytes(gate_ref, meta_sem.at[1])
        wait_bytes(xs, xsend)

    @pl.when(on_b)
    def _():
        wait_bytes(ids_m, meta_sem.at[2])
        wait_bytes(gate_m, meta_sem.at[3])
        perm[...] = slot_matrix(ids_m[...], n_group, cap)
        gate_col = gate_column(gate_m[...])
        gated = (gate_col * dy_ref[...].astype(F32)).astype(BF16)
        qs[...] = dot(perm[...], gated).astype(BF16)
        for k in range(1, n_group):
            to = peer(me, k)
            send(qs.at[block(to)], qr.at[place(k)], qsend, qrecv.at[k // per], 1, to)
        qr[place(0), :] = qs[block(me), :]
        dx_ref[...] = jnp.zeros_like(dx_ref)
        for load in loads:
            load.wait()
        for r in range(N_CHUNK):
            first = 1 if r == 0 else r * per
            wait_bytes(qr.at[pl.ds(first * cap, ((r + 1) * per - first) * cap)], qrecv.at[r])
            rows = slice(r * per * cap, (r + 1) * per * cap)
            wait_bytes(xr.at[pl.ds(r * per * cap, per * cap)], xrecv.at[r])
            for j in range(d_ff // TILE):
                cols = slice(j * TILE, (j + 1) * TILE)
                dh = dot(qr[rows, :], w2[cols, :], NT)
                a = dot(xr[rows, :], w1[:, cols])
                b = dot(xr[rows, :], w3[:, cols])
                sig = jax.nn.sigmoid(a)
                act = a * sig
                h_ref[rows, cols] = (act * b).astype(BF16)
                da_ref[rows, cols] = (dh * b * sig * (1.0 + a * (1.0 - sig))).astype(BF16)
                db_ref[rows, cols] = (dh * act).astype(BF16)
            for c in range(n_col):
                cols = slice(c * COL, (c + 1) * COL)
                dxs[c, rows, :] = (dot(da_ref[rows, :], w1[cols, :], NT) + dot(db_ref[rows, :], w3[cols, :], NT)).astype(BF16)
                for k in range(r * per, (r + 1) * per):
                    send(dxs.at[c, place(k)], dxr.at[c, block(me)], dxsend, dxrecv.at[c], 0, peer(me, k))
            os[rows, :] = dot(h_ref[rows, :], w2[...]).astype(BF16)
            for k in range(r * per, (r + 1) * per):
                if k > 0:
                    send(os.at[place(k)], yr.at[block(me)], osend, yrecv, 1, peer(me, k))
            if r == 0:
                yr[block(me), :] = os[place(0), :]
        for j in range(d_ff // TILE):
            cols = slice(j * TILE, (j + 1) * TILE)
            dw2[cols, :] = dot(h_ref[:, cols], qr[...], TN).astype(BF16)
        xt[...] = xr[...].T
        for j in range(d_ff // TILE):
            cols = slice(j * TILE, (j + 1) * TILE)
            dw1[:, cols] = dot(xt[...], da_ref[:, cols]).astype(BF16)
        others = pl.ds(0, n_rows - cap)
        wait_bytes(yr.at[others], yrecv)
        y_ref[...] = (gate_col * dot(perm[...], yr[...], TN)).astype(BF16)
        wait_bytes(qs.at[others], qsend)
        wait_bytes(dxs, dxsend)
        wait_bytes(os.at[others], osend)


def store_kernel(xt, db_ref, dw1_in, dw2_in, y_in, dx_in, dw1, dw3, dw2, y_out, dx_out, dw3_v, sem, sem3):
    stage = lax.axis_index("stage")
    d_ff = db_ref.shape[1]
    pairs = ((dw2_in, dw2), (dw1_in, dw1), (y_in, y_out), (dx_in, dx_out))
    copies = [pltpu.make_async_copy(src, dst, sem.at[i]) for i, (src, dst) in enumerate(pairs)]
    for copy in copies:
        copy.start()

    @pl.when(stage == 0)
    def _():
        copy = pltpu.make_async_copy(dw1_in, dw3, sem3.at[0])
        copy.start()
        copy.wait()

    @pl.when(stage == 1)
    def _():
        pieces = []
        for j in range(d_ff // (2 * TILE)):
            cols = pl.ds(j * 2 * TILE, 2 * TILE)
            dw3_v[:, cols] = dot(xt[...], db_ref[:, cols]).astype(BF16)
            pieces.append(pltpu.make_async_copy(dw3_v.at[:, cols], dw3.at[:, cols], sem3.at[j]))
            pieces[-1].start()
        for piece in pieces:
            piece.wait()

    for copy in copies:
        copy.wait()


def solution(mesh):
    n_group = mesh.shape["expert"]
    tok_spec = P("stage", "expert", None)
    w_spec = P("stage", "expert", None, None)

    def device_fn(tokens_in, expert_ids, gate_wts, w_gate, w_up, w_down, grad_out):
        n_tok, d_model = tokens_in.shape[1:]
        d_ff = w_gate.shape[3]
        cap = 3 * n_tok // (2 * n_group)
        n_rows = n_group * cap
        vmem = pl.BlockSpec(memory_space=pltpu.VMEM)
        hbm = pl.BlockSpec(memory_space=pl.ANY)
        blocks = pltpu.VMEM((n_rows, d_model), BF16)
        pieces = pltpu.VMEM((d_model // COL, n_rows, COL), BF16)
        hidden = pltpu.VMEM((n_rows, d_ff), BF16)
        up = pltpu.VMEM((d_model, d_ff), BF16)
        down = pltpu.VMEM((d_ff, d_model), BF16)
        tok = pltpu.VMEM((n_tok, d_model), BF16)
        dma = pltpu.SemaphoreType.DMA
        y, dx, xt, db, dw1, dw2 = pl.pallas_call(
            functools.partial(exchange_kernel, n_group, cap),
            out_shape=(tok, tok, pltpu.VMEM((d_model, n_rows), BF16), hidden, up, down),
            in_specs=[vmem] * 4 + [hbm] * 3,
            out_specs=(vmem,) * 6,
            scratch_shapes=[
                up, up, down, blocks, blocks, hidden, hidden,
                pltpu.VMEM((n_rows, n_tok), BF16),
                blocks, blocks, pieces, pieces, blocks, blocks,
                pltpu.VMEM((1, n_tok), jnp.int32),
                pltpu.VMEM((1, n_tok), F32),
                dma((3,)),
                dma((4,)),
                dma(()),
                dma((N_CHUNK,)),
                dma(()),
                dma((N_CHUNK,)),
                dma(()),
                dma((d_model // COL,)),
                dma(()),
                dma(()),
            ],
            compiler_params=pltpu.CompilerParams(
                collective_id=0, has_side_effects=True, vmem_limit_bytes=40 * 2**20
            ),
            name="exchange",
        )(
            expert_ids.reshape(1, n_tok), gate_wts.reshape(1, n_tok), tokens_in[0], grad_out[0],
            w_gate[0, 0], w_up[0, 0], w_down[0, 0],
        )
        held = [pltpu.with_memory_space_constraint(v, pltpu.VMEM) for v in (xt, db, dw1, dw2, y, dx)]
        dw1, dw3, dw2, y, dx = pl.pallas_call(
            store_kernel,
            out_shape=(
                jax.ShapeDtypeStruct((d_model, d_ff), BF16),
                jax.ShapeDtypeStruct((d_model, d_ff), BF16),
                jax.ShapeDtypeStruct((d_ff, d_model), BF16),
                jax.ShapeDtypeStruct((n_tok, d_model), BF16),
                jax.ShapeDtypeStruct((n_tok, d_model), BF16),
            ),
            in_specs=[vmem] * 6,
            out_specs=(hbm,) * 5,
            scratch_shapes=[up, dma((4,)), dma((d_ff // (2 * TILE),))],
            compiler_params=pltpu.CompilerParams(vmem_limit_bytes=16 * 2**20),
            name="store",
        )(*held)
        return y[None], dx[None], dw1[None, None], dw3[None, None], dw2[None, None]

    return jax.shard_map(
        device_fn,
        mesh=mesh,
        in_specs=(tok_spec, tok_spec, tok_spec, w_spec, w_spec, w_spec, tok_spec),
        out_specs=(tok_spec, tok_spec, w_spec, w_spec, w_spec),
        check_vma=False,
    )
```

time: 63.9 us -> 55.9 us (0.87)
  the two profiles are of different devices: /device:TPU:9 before, /device:TPU:11 now
where the time goes in v2:
time: 55.9 us; the launch traced here: 55.7 us
  Pallas kernels  51.5 us (92%)
  local copies, waits for them, and re-layouts  3.34 us (6%)
  between operations  0.83 us (1%)
    pallas_call x1, Pallas kernels, device_fn(): pl.pallas_call(functools.partial(exchange_kernel, n_group, cap), out_shap...  46.1 us
    pallas_call x1, Pallas kernels, device_fn(): pl.pallas_call(store_kernel, out_shape=(jax.ShapeDtypeStruct((d_model, d_...  5.37 us
    unnamed x8, local copies, waits for them, and re-layouts  3.34 us

profile of v2, /device:TPU:11, one launch (start us, length us, event | category | flops | bytes accessed | tf_op | source)
XLA Modules:
  0.0 55.7 jit_solution(13424445373690636803)
XLA Ops:
  0.6 0.0 copy-start
  0.6 1.0 %copy-done = bf16[1,256,768]{2,1,0:T(8,128)(2,1)S(1)} copy-done((bf16[1,256,768]{2,1,0:T(8,128)(2,1)S(1)}, bf16[1,256,768]{2,1,0:T(8,128)(2,1)}, u32[]{:S(2)}) %copy-start) | copy-done | bytes 393240
  1.6 0.0 copy-start.1
  1.6 1.0 %copy-done.1 = bf16[1,256,768]{2,1,0:T(8,128)(2,1)S(1)} copy-done((bf16[1,256,768]{2,1,0:T(8,128)(2,1)S(1)}, bf16[1,256,768]{2,1,0:T(8,128)(2,1)}, u32[]{:S(2)}) %copy-start.1) | copy-done | bytes 393240
  2.6 0.0 copy-start.2
  2.6 0.7 %copy-done.2 = s32[1,256,1]{1,2,0:T(1,128)S(1)} copy-done((s32[1,256,1]{1,2,0:T(1,128)S(1)}, s32[1,256,1]{1,2,0:T(1,128)}, u32[]{:S(2)}) %copy-start.2) | copy-done | bytes 1048
  3.3 0.0 copy-start.3
  3.3 0.7 %copy-done.3 = f32[1,256,1]{1,2,0:T(1,128)S(1)} copy-done((f32[1,256,1]{1,2,0:T(1,128)S(1)}, f32[1,256,1]{1,2,0:T(1,128)}, u32[]{:S(2)}) %copy-start.3) | copy-done | bytes 1048
  4.0 46.1 %exchange.1 = (bf16[256,768]{1,0:T(8,128)(2,1)S(1)}, bf16[256,768]{1,0:T(8,128)(2,1)S(1)}, bf16[768,384]{1,0:T(8,128)(2,1)S(1)}, bf16[384,3072]{1,0:T(8,128)(2,1...) custom-call(s32[1,256]{1,0:T(1,128)S(1)} %bitcast.14, f32[1,256]{1,0:T(1,128)S(1)} %bitcast.15, ...), custom_call_target="tpu_custom_call" | custom-call | tf_op jit(solution)/shard_map/exchange/pallas_call | solution.py:220
  50.1 5.4 %store.1 = (bf16[768,3072]{1,0:T(8,128)(2,1)}, bf16[768,3072]{1,0:T(8,128)(2,1)}, bf16[3072,768]{1,0:T(8,128)(2,1)}, bf16[256,768]{1,0:T(8,128)(2,1)}, bf16[256,768]{1,0:T(8,128)(2,1)}) custom-call(bf16[768,384]{1,0:T(8,128)(2,1)S(1)} %get-tuple-element.16.xt, bf16[384,3072]{1,0:T(8,128)(2,1)S(1)} %get-tuple-element.17.db_ref, ...), custom_call_target="tpu_custom_call" | custom-call | tf_op jit(solution)/shard_map/store/pallas_call | solution.py:251
Async XLA Ops:
  0.6 1.0 %copy-start = (bf16[1,256,768]{2,1,0:T(8,128)(2,1)S(1)}, bf16[1,256,768]{2,1,0:T(8,128)(2,1)}, u32[]{:S(2)}) copy-start(bf16[1,256,768]{2,1,0:T(8,128)(2,1)} %param.7) | copy-start | bytes 1179652
  1.6 1.0 %copy-start.1 = (bf16[1,256,768]{2,1,0:T(8,128)(2,1)S(1)}, bf16[1,256,768]{2,1,0:T(8,128)(2,1)}, u32[]{:S(2)}) copy-start(bf16[1,256,768]{2,1,0:T(8,128)(2,1)} %param.13) | copy-start | bytes 1179652
  2.6 0.7 %copy-start.2 = (s32[1,256,1]{1,2,0:T(1,128)S(1)}, s32[1,256,1]{1,2,0:T(1,128)}, u32[]{:S(2)}) copy-start(s32[1,256,1]{1,2,0:T(1,128)} %param.8) | copy-start | bytes 3076
  3.3 0.7 %copy-start.3 = (f32[1,256,1]{1,2,0:T(1,128)S(1)}, f32[1,256,1]{1,2,0:T(1,128)}, u32[]{:S(2)}) copy-start(f32[1,256,1]{1,2,0:T(1,128)} %param.9) | copy-start | bytes 3076

commit v3 on v2

--- a/solution.py
+++ b/solution.py
@@ -13,6 +13,8 @@
 COL = 256
 TILE = 256
 N_CHUNK = 2
+WIDE = 768
+WINDOW = 1
 NT = (((1,), (1,)), ((), ()))
 TN = (((0,), (0,)), ((), ()))
 PEERS = ((0, 0, 0), (0, 0, 1), (1, 1, 0), (1, 1, 1), (0, 1, 0), (0, 1, 1), (1, 0, 0), (1, 0, 1))
@@ -47,10 +49,10 @@
 
 def exchange_kernel(
     n_group, cap,
-    ids_ref, gate_ref, x_ref, dy_ref, w1_hbm, w3_hbm, w2_hbm,
+    ids_hbm, gate_hbm, x_hbm, dy_hbm, w1_hbm, w3_hbm, w2_hbm,
     y_ref, dx_ref, xt, db_ref, dw1, dw2,
-    w1, w3, w2, xr, qr, h_ref, da_ref, perm, xs, qs, dxs, dxr, os, yr, ids_m, gate_m,
-    w_sem, meta_sem, xsend, xrecv, qsend, qrecv, dxsend, dxrecv, osend, yrecv,
+    w1, w3, w2, xr, qr, h_ref, da_ref, perm, xs, qs, dxs, dxr, os, yr, ids_m, gate_m, tok_v,
+    w_sem, in_sem, meta_sem, xsend, xrecv, qsend, qrecv, dxsend, dxrecv, osend, yrecv,
 ):
     stage = lax.axis_index("stage")
     me = lax.axis_index("expert")
@@ -84,34 +86,54 @@
         )
     loads = [pltpu.make_async_copy(src, dst, w_sem.at[i]) for i, (src, dst) in enumerate(((w2_hbm, w2), (w1_hbm, w1), (w3_hbm, w3)))]
 
+    ids_load = pltpu.make_async_copy(ids_hbm, ids_m, in_sem.at[0])
+    gate_load = pltpu.make_async_copy(gate_hbm, gate_m, in_sem.at[1])
+    x_load = pltpu.make_async_copy(x_hbm, tok_v, in_sem.at[2])
+    dy_load = pltpu.make_async_copy(dy_hbm, tok_v, in_sem.at[2])
+
     @pl.when(on_b)
     def _():
+        dy_load.start()
         for load in loads:
             load.start()
 
     @pl.when(on_a)
     def _():
-        perm[...] = slot_matrix(ids_ref[...], n_group, cap)
-        xs[...] = dot(perm[...], x_ref[...]).astype(BF16)
+        ids_load.start()
+        gate_load.start()
+        x_load.start()
+        ids_load.wait()
+        gate_load.wait()
+        perm[...] = slot_matrix(ids_m[...], n_group, cap)
+        x_load.wait()
+        xs[...] = dot(perm[...], tok_v[...]).astype(BF16)
 
     pl.semaphore_wait(barrier, 2 * n_group - 1)
 
     @pl.when(on_a)
     def _():
-        send(ids_ref, ids_m, meta_sem.at[0], meta_sem.at[2], 1, me)
-        send(gate_ref, gate_m, meta_sem.at[1], meta_sem.at[3], 1, me)
+        send(ids_m, ids_m, meta_sem.at[0], meta_sem.at[2], 1, me)
+        send(gate_m, gate_m, meta_sem.at[1], meta_sem.at[3], 1, me)
         for k in range(n_group):
             to = peer(me, k)
-            send(xs.at[block(to)], xr.at[place(k)], xsend, xrecv.at[k // per], 1, to)
+            if k >= WINDOW:
+                wait_bytes(xs.at[place(0)], xsend.at[k - WINDOW])
+            send(xs.at[block(to)], xr.at[place(k)], xsend.at[k], xrecv.at[k // per], 1, to)
+        for k in range(n_group - WINDOW, n_group):
+            wait_bytes(xs.at[place(0)], xsend.at[k])
         y_ref[...] = jnp.zeros_like(y_ref)
-        dw1[...] = jnp.zeros_like(dw1)
-        dw2[...] = jnp.zeros_like(dw2)
+
+        @pl.loop(0, d_ff // WIDE)
+        def _(j):
+            cols = pl.ds(pl.multiple_of(j * WIDE, WIDE), WIDE)
+            dw1[:, cols] = jnp.zeros((d_model, WIDE), BF16)
+            dw2[cols, :] = jnp.zeros((WIDE, d_model), BF16)
+
         for c in range(n_col):
             wait_bytes(dxr.at[c], dxrecv.at[c])
             dx_ref[:, c * COL:(c + 1) * COL] = dot(perm[...], dxr[c], TN).astype(BF16)
-        wait_bytes(ids_ref, meta_sem.at[0])
-        wait_bytes(gate_ref, meta_sem.at[1])
-        wait_bytes(xs, xsend)
+        wait_bytes(ids_m, meta_sem.at[0])
+        wait_bytes(gate_m, meta_sem.at[1])
 
     @pl.when(on_b)
     def _():
@@ -119,13 +141,17 @@
         wait_bytes(gate_m, meta_sem.at[3])
         perm[...] = slot_matrix(ids_m[...], n_group, cap)
         gate_col = gate_column(gate_m[...])
-        gated = (gate_col * dy_ref[...].astype(F32)).astype(BF16)
+        dy_load.wait()
+        gated = (gate_col * tok_v[...].astype(F32)).astype(BF16)
         qs[...] = dot(perm[...], gated).astype(BF16)
-        for k in range(1, n_group):
-            to = peer(me, k)
-            send(qs.at[block(to)], qr.at[place(k)], qsend, qrecv.at[k // per], 1, to)
-        qr[place(0), :] = qs[block(me), :]
-        dx_ref[...] = jnp.zeros_like(dx_ref)
+        for r in range(N_CHUNK):
+            for k in range(max(1, r * per), (r + 1) * per):
+                to = peer(me, k)
+                send(qs.at[block(to)], qr.at[place(k)], qsend.at[r], qrecv.at[r], 1, to)
+            if r == 0:
+                qr[place(0), :] = qs[block(me), :]
+                dx_ref[...] = jnp.zeros_like(dx_ref)
+                wait_bytes(qs.at[pl.ds(0, (per - 1) * cap)], qsend.at[r])
         for load in loads:
             load.wait()
         for r in range(N_CHUNK):
@@ -143,28 +169,39 @@
                 h_ref[rows, cols] = (act * b).astype(BF16)
                 da_ref[rows, cols] = (dh * b * sig * (1.0 + a * (1.0 - sig))).astype(BF16)
                 db_ref[rows, cols] = (dh * act).astype(BF16)
-            for c in range(n_col):
-                cols = slice(c * COL, (c + 1) * COL)
+
+            @pl.loop(0, n_col)
+            def _(c):
+                cols = pl.ds(pl.multiple_of(c * COL, COL), COL)
                 dxs[c, rows, :] = (dot(da_ref[rows, :], w1[cols, :], NT) + dot(db_ref[rows, :], w3[cols, :], NT)).astype(BF16)
                 for k in range(r * per, (r + 1) * per):
                     send(dxs.at[c, place(k)], dxr.at[c, block(me)], dxsend, dxrecv.at[c], 0, peer(me, k))
-            os[rows, :] = dot(h_ref[rows, :], w2[...]).astype(BF16)
+
+            @pl.loop(0, n_col)
+            def _(c):
+                cols = pl.ds(pl.multiple_of(c * COL, COL), COL)
+                os[rows, cols] = dot(h_ref[rows, :], w2[:, cols]).astype(BF16)
+
             for k in range(r * per, (r + 1) * per):
                 if k > 0:
                     send(os.at[place(k)], yr.at[block(me)], osend, yrecv, 1, peer(me, k))
             if r == 0:
                 yr[block(me), :] = os[place(0), :]
-        for j in range(d_ff // TILE):
-            cols = slice(j * TILE, (j + 1) * TILE)
+        @pl.loop(0, d_ff // WIDE)
+        def _(j):
+            cols = pl.ds(pl.multiple_of(j * WIDE, WIDE), WIDE)
             dw2[cols, :] = dot(h_ref[:, cols], qr[...], TN).astype(BF16)
         xt[...] = xr[...].T
-        for j in range(d_ff // TILE):
-            cols = slice(j * TILE, (j + 1) * TILE)
+
+        @pl.loop(0, d_ff // WIDE)
+        def _(j):
+            cols = pl.ds(pl.multiple_of(j * WIDE, WIDE), WIDE)
             dw1[:, cols] = dot(xt[...], da_ref[:, cols]).astype(BF16)
+
         others = pl.ds(0, n_rows - cap)
         wait_bytes(yr.at[others], yrecv)
         y_ref[...] = (gate_col * dot(perm[...], yr[...], TN)).astype(BF16)
-        wait_bytes(qs.at[others], qsend)
+        wait_bytes(qs.at[pl.ds(0, per * cap)], qsend.at[1])
         wait_bytes(dxs, dxsend)
         wait_bytes(os.at[others], osend)
 
@@ -220,7 +257,7 @@
         y, dx, xt, db, dw1, dw2 = pl.pallas_call(
             functools.partial(exchange_kernel, n_group, cap),
             out_shape=(tok, tok, pltpu.VMEM((d_model, n_rows), BF16), hidden, up, down),
-            in_specs=[vmem] * 4 + [hbm] * 3,
+            in_specs=[hbm] * 7,
             out_specs=(vmem,) * 6,
             scratch_shapes=[
                 up, up, down, blocks, blocks, hidden, hidden,
@@ -228,11 +265,13 @@
                 blocks, blocks, pieces, pieces, blocks, blocks,
                 pltpu.VMEM((1, n_tok), jnp.int32),
                 pltpu.VMEM((1, n_tok), F32),
+                tok,
+                dma((3,)),
                 dma((3,)),
                 dma((4,)),
-                dma(()),
+                dma((n_group,)),
                 dma((N_CHUNK,)),
-                dma(()),
+                dma((N_CHUNK,)),
                 dma((N_CHUNK,)),
                 dma(()),
                 dma((d_model // COL,)),
@@ -243,10 +282,10 @@
                 collective_id=0, has_side_effects=True, vmem_limit_bytes=40 * 2**20
             ),
             name="exchange",
-        )(
+        )(*(pltpu.with_memory_space_constraint(v, pltpu.HBM) for v in (
             expert_ids.reshape(1, n_tok), gate_wts.reshape(1, n_tok), tokens_in[0], grad_out[0],
             w_gate[0, 0], w_up[0, 0], w_down[0, 0],
-        )
+        )))
         held = [pltpu.with_memory_space_constraint(v, pltpu.VMEM) for v in (xt, db, dw1, dw2, y, dx)]
         dw1, dw3, dw2, y, dx = pl.pallas_call(
             store_kernel,

time: 55.9 us -> 44.5 us (0.80)
  the two profiles are of different devices: /device:TPU:11 before, /device:TPU:9 now
where the time goes in v3:
time: 44.5 us; the launch traced here: 44 us
  Pallas kernels  43.4 us (98%)
  between operations  0.64 us (1%)
    pallas_call x1, Pallas kernels, device_fn(): pl.pallas_call(functools.partial(exchange_kernel, n_group, cap), out_shap...  38 us
    pallas_call x1, Pallas kernels, device_fn(): pl.pallas_call(store_kernel, out_shape=(jax.ShapeDtypeStruct((d_model, d_...  5.37 us

profile of v3, /device:TPU:9, one launch (start us, length us, event | category | flops | bytes accessed | tf_op | source)
XLA Modules:
  0.0 44.0 jit_solution(13448824491757750605)
XLA Ops:
  0.6 38.0 %exchange.1 = (bf16[256,768]{1,0:T(8,128)(2,1)S(1)}, bf16[256,768]{1,0:T(8,128)(2,1)S(1)}, bf16[768,384]{1,0:T(8,128)(2,1)S(1)}, bf16[384,3072]{1,0:T(8,128)(2,1...) custom-call(s32[1,256]{1,0:T(1,128)} %bitcast.17, f32[1,256]{1,0:T(1,128)} %bitcast.18, ...), custom_call_target="tpu_custom_call" | custom-call | tf_op jit(solution)/shard_map/exchange/pallas_call | solution.py:257
  38.6 5.4 %store.1 = (bf16[768,3072]{1,0:T(8,128)(2,1)}, bf16[768,3072]{1,0:T(8,128)(2,1)}, bf16[3072,768]{1,0:T(8,128)(2,1)}, bf16[256,768]{1,0:T(8,128)(2,1)}, bf16[256,768]{1,0:T(8,128)(2,1)}) custom-call(bf16[768,384]{1,0:T(8,128)(2,1)S(1)} %get-tuple-element.16.xt, bf16[384,3072]{1,0:T(8,128)(2,1)S(1)} %get-tuple-element.17.db_ref, ...), custom_call_target="tpu_custom_call" | custom-call | tf_op jit(solution)/shard_map/store/pallas_call | solution.py:290

commit v4 on v3

--- a/solution.py
+++ b/solution.py
@@ -11,10 +11,13 @@
 BF16 = jnp.bfloat16
 F32 = jnp.float32
 COL = 256
+PIECE = 512
 TILE = 256
-N_CHUNK = 2
+CHUNKS = ((0, 4), (4, 8))
+HERE = 1536
 WIDE = 768
-WINDOW = 1
+THIRD = 16
+WINDOWS = (9, 4)
 NT = (((1,), (1,)), ((), ()))
 TN = (((0,), (0,)), ((), ()))
 PEERS = ((0, 0, 0), (0, 0, 1), (1, 1, 0), (1, 1, 1), (0, 1, 0), (0, 1, 1), (1, 0, 0), (1, 0, 1))
@@ -50,8 +53,8 @@
 def exchange_kernel(
     n_group, cap,
     ids_hbm, gate_hbm, x_hbm, dy_hbm, w1_hbm, w3_hbm, w2_hbm,
-    y_ref, dx_ref, xt, db_ref, dw1, dw2,
-    w1, w3, w2, xr, qr, h_ref, da_ref, perm, xs, qs, dxs, dxr, os, yr, ids_m, gate_m, tok_v,
+    y_ref, dx_ref, xt, da_ref, db_ref, dw1, dw2,
+    w1, w3, w2, w1t, w3t, w2t, xr, qr, h_ref, perm, xs, qs, dxs, dxr, os, yr, ids_m, gate_m, tok_v,
     w_sem, in_sem, meta_sem, xsend, xrecv, qsend, qrecv, dxsend, dxrecv, osend, yrecv,
 ):
     stage = lax.axis_index("stage")
@@ -59,7 +62,7 @@
     n_rows = n_group * cap
     d_model, d_ff = w1.shape
     n_col = d_model // COL
-    per = n_group // N_CHUNK
+    chunk_of = [r for r, (lo, hi) in enumerate(CHUNKS) for _ in range(lo, hi)]
     on_a = stage == 0
     on_b = stage == 1
 
@@ -114,20 +117,33 @@
     def _():
         send(ids_m, ids_m, meta_sem.at[0], meta_sem.at[2], 1, me)
         send(gate_m, gate_m, meta_sem.at[1], meta_sem.at[3], 1, me)
-        for k in range(n_group):
-            to = peer(me, k)
-            if k >= WINDOW:
-                wait_bytes(xs.at[place(0)], xsend.at[k - WINDOW])
-            send(xs.at[block(to)], xr.at[place(k)], xsend.at[k], xrecv.at[k // per], 1, to)
-        for k in range(n_group - WINDOW, n_group):
-            wait_bytes(xs.at[place(0)], xsend.at[k])
+        n_third = cap // THIRD
+
+        def send_x(window):
+            for p in range(n_group * n_third):
+                k, part = divmod(p, n_third)
+                to = peer(me, k)
+                if p >= window:
+                    wait_bytes(xs.at[pl.ds(0, THIRD)], xsend.at[p % window])
+                src = pl.ds(pl.multiple_of(to * cap + part * THIRD, THIRD), THIRD)
+                dst = pl.ds(k * cap + part * THIRD, THIRD)
+                send(xs.at[src], xr.at[dst], xsend.at[p % window], xrecv.at[chunk_of[k]], 1, to)
+            for p in range(window):
+                wait_bytes(xs.at[pl.ds(0, THIRD)], xsend.at[p])
+
+        for core, window in enumerate(WINDOWS):
+            pl.when(lax.rem(me, 2) == core)(functools.partial(send_x, window))
         y_ref[...] = jnp.zeros_like(y_ref)
 
         @pl.loop(0, d_ff // WIDE)
+        def _(j):
+            cols = pl.ds(pl.multiple_of(j * WIDE, WIDE), WIDE)
+            dw2[cols, :] = jnp.zeros((WIDE, d_model), BF16)
+
+        @pl.loop(0, HERE // WIDE)
         def _(j):
             cols = pl.ds(pl.multiple_of(j * WIDE, WIDE), WIDE)
             dw1[:, cols] = jnp.zeros((d_model, WIDE), BF16)
-            dw2[cols, :] = jnp.zeros((WIDE, d_model), BF16)
 
         for c in range(n_col):
             wait_bytes(dxr.at[c], dxrecv.at[c])
@@ -137,6 +153,18 @@
 
     @pl.when(on_b)
     def _():
+        eye = (
+            lax.broadcasted_iota(jnp.int32, (TILE, TILE), 0) == lax.broadcasted_iota(jnp.int32, (TILE, TILE), 1)
+        ).astype(BF16)
+        loads[0].wait()
+
+        @pl.loop(0, d_ff // WIDE)
+        def _(j):
+            for c in range(n_col):
+                wide = pl.ds(pl.multiple_of(j * WIDE, WIDE), WIDE)
+                cols = slice(c * COL, (c + 1) * COL)
+                w2t[cols, wide] = dot(eye, w2[wide, cols], NT).astype(BF16)
+
         wait_bytes(ids_m, meta_sem.at[2])
         wait_bytes(gate_m, meta_sem.at[3])
         perm[...] = slot_matrix(ids_m[...], n_group, cap)
@@ -144,24 +172,33 @@
         dy_load.wait()
         gated = (gate_col * tok_v[...].astype(F32)).astype(BF16)
         qs[...] = dot(perm[...], gated).astype(BF16)
-        for r in range(N_CHUNK):
-            for k in range(max(1, r * per), (r + 1) * per):
+
+        def send_q(r):
+            for k in range(max(1, CHUNKS[r][0]), CHUNKS[r][1]):
                 to = peer(me, k)
-                send(qs.at[block(to)], qr.at[place(k)], qsend.at[r], qrecv.at[r], 1, to)
-            if r == 0:
-                qr[place(0), :] = qs[block(me), :]
-                dx_ref[...] = jnp.zeros_like(dx_ref)
-                wait_bytes(qs.at[pl.ds(0, (per - 1) * cap)], qsend.at[r])
-        for load in loads:
+                send(qs.at[block(to)], qr.at[place(k)], qsend, qrecv.at[r], 1, to)
+
+        send_q(0)
+        for load, src, dst in ((loads[1], w1, w1t), (loads[2], w3, w3t)):
             load.wait()
-        for r in range(N_CHUNK):
-            first = 1 if r == 0 else r * per
-            wait_bytes(qr.at[pl.ds(first * cap, ((r + 1) * per - first) * cap)], qrecv.at[r])
-            rows = slice(r * per * cap, (r + 1) * per * cap)
-            wait_bytes(xr.at[pl.ds(r * per * cap, per * cap)], xrecv.at[r])
+
+            @pl.loop(0, d_ff // WIDE)
+            def _(j):
+                for i in range(WIDE // TILE):
+                    tile = pl.ds(pl.multiple_of(j * WIDE + i * TILE, TILE), TILE)
+                    dst[tile, :] = dot(eye, src[:, tile], NT).astype(BF16)
+
+        send_q(1)
+        qr[place(0), :] = qs[block(me), :]
+        dx_ref[...] = jnp.zeros_like(dx_ref)
+        for r, (lo, hi) in enumerate(CHUNKS):
+            first = max(1, lo)
+            wait_bytes(qr.at[pl.ds(first * cap, (hi - first) * cap)], qrecv.at[r])
+            rows = slice(lo * cap, hi * cap)
+            wait_bytes(xr.at[pl.ds(lo * cap, (hi - lo) * cap)], xrecv.at[r])
             for j in range(d_ff // TILE):
                 cols = slice(j * TILE, (j + 1) * TILE)
-                dh = dot(qr[rows, :], w2[cols, :], NT)
+                dh = dot(qr[rows, :], w2t[:, cols])
                 a = dot(xr[rows, :], w1[:, cols])
                 b = dot(xr[rows, :], w3[:, cols])
                 sig = jax.nn.sigmoid(a)
@@ -173,8 +210,8 @@
             @pl.loop(0, n_col)
             def _(c):
                 cols = pl.ds(pl.multiple_of(c * COL, COL), COL)
-                dxs[c, rows, :] = (dot(da_ref[rows, :], w1[cols, :], NT) + dot(db_ref[rows, :], w3[cols, :], NT)).astype(BF16)
-                for k in range(r * per, (r + 1) * per):
+                dxs[c, rows, :] = (dot(da_ref[rows, :], w1t[:, cols]) + dot(db_ref[rows, :], w3t[:, cols])).astype(BF16)
+                for k in range(lo, hi):
                     send(dxs.at[c, place(k)], dxr.at[c, block(me)], dxsend, dxrecv.at[c], 0, peer(me, k))
 
             @pl.loop(0, n_col)
@@ -182,7 +219,7 @@
                 cols = pl.ds(pl.multiple_of(c * COL, COL), COL)
                 os[rows, cols] = dot(h_ref[rows, :], w2[:, cols]).astype(BF16)
 
-            for k in range(r * per, (r + 1) * per):
+            for k in range(lo, hi):
                 if k > 0:
                     send(os.at[place(k)], yr.at[block(me)], osend, yrecv, 1, peer(me, k))
             if r == 0:
@@ -193,7 +230,7 @@
             dw2[cols, :] = dot(h_ref[:, cols], qr[...], TN).astype(BF16)
         xt[...] = xr[...].T
 
-        @pl.loop(0, d_ff // WIDE)
+        @pl.loop(0, HERE // WIDE)
         def _(j):
             cols = pl.ds(pl.multiple_of(j * WIDE, WIDE), WIDE)
             dw1[:, cols] = dot(xt[...], da_ref[:, cols]).astype(BF16)
@@ -201,33 +238,38 @@
         others = pl.ds(0, n_rows - cap)
         wait_bytes(yr.at[others], yrecv)
         y_ref[...] = (gate_col * dot(perm[...], yr[...], TN)).astype(BF16)
-        wait_bytes(qs.at[pl.ds(0, per * cap)], qsend.at[1])
+        wait_bytes(qs.at[others], qsend)
         wait_bytes(dxs, dxsend)
         wait_bytes(os.at[others], osend)
 
 
-def store_kernel(xt, db_ref, dw1_in, dw2_in, y_in, dx_in, dw1, dw3, dw2, y_out, dx_out, dw3_v, sem, sem3):
+def store_kernel(xt, da_ref, db_ref, dw1_in, dw2_in, y_in, dx_in, dw1, dw3, dw2, y_out, dx_out, dw1_v, dw3_v, sem, piece_sem):
     stage = lax.axis_index("stage")
     d_ff = db_ref.shape[1]
-    pairs = ((dw2_in, dw2), (dw1_in, dw1), (y_in, y_out), (dx_in, dx_out))
+    pairs = ((dw2_in, dw2), (dw1_in, dw1.at[:, pl.ds(0, HERE)]), (y_in, y_out), (dx_in, dx_out))
     copies = [pltpu.make_async_copy(src, dst, sem.at[i]) for i, (src, dst) in enumerate(pairs)]
     for copy in copies:
         copy.start()
 
     @pl.when(stage == 0)
     def _():
-        copy = pltpu.make_async_copy(dw1_in, dw3, sem3.at[0])
-        copy.start()
-        copy.wait()
+        places = [dw1.at[:, pl.ds(HERE, d_ff - HERE)], dw3.at[:, pl.ds(0, HERE)], dw3.at[:, pl.ds(HERE, d_ff - HERE)]]
+        zeros = [pltpu.make_async_copy(dw1_in.at[:, pl.ds(0, dst.shape[1])], dst, piece_sem.at[i]) for i, dst in enumerate(places)]
+        for copy in zeros:
+            copy.start()
+        for copy in zeros:
+            copy.wait()
 
     @pl.when(stage == 1)
     def _():
         pieces = []
-        for j in range(d_ff // (2 * TILE)):
-            cols = pl.ds(j * 2 * TILE, 2 * TILE)
-            dw3_v[:, cols] = dot(xt[...], db_ref[:, cols]).astype(BF16)
-            pieces.append(pltpu.make_async_copy(dw3_v.at[:, cols], dw3.at[:, cols], sem3.at[j]))
-            pieces[-1].start()
+        for grad, held, out, skip in ((da_ref, dw1_v, dw1, HERE), (db_ref, dw3_v, dw3, 0)):
+            for j in range((d_ff - skip) // PIECE):
+                here = pl.ds(j * PIECE, PIECE)
+                there = pl.ds(skip + j * PIECE, PIECE)
+                held[:, here] = dot(xt[...], grad[:, there]).astype(BF16)
+                pieces.append(pltpu.make_async_copy(held.at[:, here], out.at[:, there], piece_sem.at[len(pieces)]))
+                pieces[-1].start()
         for piece in pieces:
             piece.wait()
 
@@ -254,13 +296,13 @@
         down = pltpu.VMEM((d_ff, d_model), BF16)
         tok = pltpu.VMEM((n_tok, d_model), BF16)
         dma = pltpu.SemaphoreType.DMA
-        y, dx, xt, db, dw1, dw2 = pl.pallas_call(
+        y, dx, xt, da, db, dw1, dw2 = pl.pallas_call(
             functools.partial(exchange_kernel, n_group, cap),
-            out_shape=(tok, tok, pltpu.VMEM((d_model, n_rows), BF16), hidden, up, down),
+            out_shape=(tok, tok, pltpu.VMEM((d_model, n_rows), BF16), hidden, hidden, pltpu.VMEM((d_model, HERE), BF16), down),
             in_specs=[hbm] * 7,
-            out_specs=(vmem,) * 6,
+            out_specs=(vmem,) * 7,
             scratch_shapes=[
-                up, up, down, blocks, blocks, hidden, hidden,
+                up, up, down, down, down, up, blocks, blocks, hidden,
                 pltpu.VMEM((n_rows, n_tok), BF16),
                 blocks, blocks, pieces, pieces, blocks, blocks,
                 pltpu.VMEM((1, n_tok), jnp.int32),
@@ -269,24 +311,24 @@
                 dma((3,)),
                 dma((3,)),
                 dma((4,)),
-                dma((n_group,)),
-                dma((N_CHUNK,)),
-                dma((N_CHUNK,)),
-                dma((N_CHUNK,)),
+                dma((max(WINDOWS),)),
+                dma((len(CHUNKS),)),
+                dma(()),
+                dma((len(CHUNKS),)),
                 dma(()),
                 dma((d_model // COL,)),
                 dma(()),
                 dma(()),
             ],
             compiler_params=pltpu.CompilerParams(
-                collective_id=0, has_side_effects=True, vmem_limit_bytes=40 * 2**20
+                collective_id=0, has_side_effects=True, vmem_limit_bytes=48 * 2**20
             ),
             name="exchange",
         )(*(pltpu.with_memory_space_constraint(v, pltpu.HBM) for v in (
             expert_ids.reshape(1, n_tok), gate_wts.reshape(1, n_tok), tokens_in[0], grad_out[0],
             w_gate[0, 0], w_up[0, 0], w_down[0, 0],
         )))
-        held = [pltpu.with_memory_space_constraint(v, pltpu.VMEM) for v in (xt, db, dw1, dw2, y, dx)]
+        held = [pltpu.with_memory_space_constraint(v, pltpu.VMEM) for v in (xt, da, db, dw1, dw2, y, dx)]
         dw1, dw3, dw2, y, dx = pl.pallas_call(
             store_kernel,
             out_shape=(
@@ -296,9 +338,9 @@
                 jax.ShapeDtypeStruct((n_tok, d_model), BF16),
                 jax.ShapeDtypeStruct((n_tok, d_model), BF16),
             ),
-            in_specs=[vmem] * 6,
+            in_specs=[vmem] * 7,
             out_specs=(hbm,) * 5,
-            scratch_shapes=[up, dma((4,)), dma((d_ff // (2 * TILE),))],
+            scratch_shapes=[pltpu.VMEM((d_model, d_ff - HERE), BF16), up, dma((4,)), dma(((2 * d_ff - HERE) // PIECE,))],
             compiler_params=pltpu.CompilerParams(vmem_limit_bytes=16 * 2**20),
             name="store",
         )(*held)

time: 44.5 us -> 41.4 us (0.930)
  Pallas kernels: 43.4 us -> 40.5 us
    pallas_call x1, Pallas kernels: 38 us -> 35.1 us  [device_fn(): pl.pallas_call(functools.partial(exchange_kernel, n_group, cap), out_shap...]
where the time goes in v4:
time: 41.4 us; the launch traced here: 41.3 us
  Pallas kernels  40.5 us (98%)
  between operations  0.8 us (2%)
    pallas_call x1, Pallas kernels, device_fn(): pl.pallas_call(functools.partial(exchange_kernel, n_group, cap), out_shap...  35.1 us
    pallas_call x1, Pallas kernels, device_fn(): pl.pallas_call(store_kernel, out_shape=(jax.ShapeDtypeStruct((d_model, d_...  5.39 us

profile of v4, /device:TPU:9, one launch (start us, length us, event | category | flops | bytes accessed | tf_op | source)
XLA Modules:
  0.0 41.3 jit_solution(16723267597853308449)
XLA Ops:
  0.6 35.1 %exchange.1 = (bf16[256,768]{1,0:T(8,128)(2,1)S(1)}, bf16[256,768]{1,0:T(8,128)(2,1)S(1)}, bf16[768,384]{1,0:T(8,128)(2,1)S(1)}, bf16[384,3072]{1,0:T(8,128)(2,1...) custom-call(s32[1,256]{1,0:T(1,128)} %bitcast.17, ...), custom_call_target="tpu_custom_call" | custom-call | tf_op jit(solution)/shard_map/exchange/pallas_call | solution.py:299
  35.7 5.4 %store.1 = (bf16[768,3072]{1,0:T(8,128)(2,1)}, bf16[768,3072]{1,0:T(8,128)(2,1)}, bf16[3072,768]{1,0:T(8,128)(2,1)}, bf16[256,768]{1,0:T(8,128)(2,1)}, bf16[256,768]{1,0:T(8,128)(2,1)}) custom-call(bf16[768,384]{1,0:T(8,128)(2,1)S(1)} %get-tuple-element.17.xt, bf16[384,3072]{1,0:T(8,128)(2,1)S(1)} %get-tuple-element.18.da_ref, ...), custom_call_target="tpu_custom_call" | custom-call | tf_op jit(solution)/shard_map/store/pallas_call | solution.py:332

commit v5 on v4

--- a/solution.py
+++ b/solution.py
@@ -16,8 +16,6 @@
 CHUNKS = ((0, 4), (4, 8))
 HERE = 1536
 WIDE = 768
-THIRD = 16
-WINDOWS = (9, 4)
 NT = (((1,), (1,)), ((), ()))
 TN = (((0,), (0,)), ((), ()))
 PEERS = ((0, 0, 0), (0, 0, 1), (1, 1, 0), (1, 1, 1), (0, 1, 0), (0, 1, 1), (1, 0, 0), (1, 0, 1))
@@ -53,16 +51,15 @@
 def exchange_kernel(
     n_group, cap,
     ids_hbm, gate_hbm, x_hbm, dy_hbm, w1_hbm, w3_hbm, w2_hbm,
-    y_ref, dx_ref, xt, da_ref, db_ref, dw1, dw2,
-    w1, w3, w2, w1t, w3t, w2t, xr, qr, h_ref, perm, xs, qs, dxs, dxr, os, yr, ids_m, gate_m, tok_v,
-    w_sem, in_sem, meta_sem, xsend, xrecv, qsend, qrecv, dxsend, dxrecv, osend, yrecv,
+    perm, gate_m, back, xt, da_ref, db_ref, dw1, dw2,
+    w1, w3, w2, w1t, w3t, w2t, xr, qr, h_ref, xs, qs, dxs, os, ids_m, tok_v,
+    w_sem, in_sem, meta_sem, xsend, xrecv, qsend, qrecv, dxsend, dxrecv, osend, yrecv, pair_sem,
 ):
     stage = lax.axis_index("stage")
     me = lax.axis_index("expert")
     n_rows = n_group * cap
     d_model, d_ff = w1.shape
     n_col = d_model // COL
-    chunk_of = [r for r, (lo, hi) in enumerate(CHUNKS) for _ in range(lo, hi)]
     on_a = stage == 0
     on_b = stage == 1
 
@@ -117,23 +114,14 @@
     def _():
         send(ids_m, ids_m, meta_sem.at[0], meta_sem.at[2], 1, me)
         send(gate_m, gate_m, meta_sem.at[1], meta_sem.at[3], 1, me)
-        n_third = cap // THIRD
-
-        def send_x(window):
-            for p in range(n_group * n_third):
-                k, part = divmod(p, n_third)
+        for r, (lo, hi) in enumerate(CHUNKS):
+            for k in range(lo, hi):
                 to = peer(me, k)
-                if p >= window:
-                    wait_bytes(xs.at[pl.ds(0, THIRD)], xsend.at[p % window])
-                src = pl.ds(pl.multiple_of(to * cap + part * THIRD, THIRD), THIRD)
-                dst = pl.ds(k * cap + part * THIRD, THIRD)
-                send(xs.at[src], xr.at[dst], xsend.at[p % window], xrecv.at[chunk_of[k]], 1, to)
-            for p in range(window):
-                wait_bytes(xs.at[pl.ds(0, THIRD)], xsend.at[p])
-
-        for core, window in enumerate(WINDOWS):
-            pl.when(lax.rem(me, 2) == core)(functools.partial(send_x, window))
-        y_ref[...] = jnp.zeros_like(y_ref)
+                send(xs.at[block(to)], xr.at[place(k)], xsend.at[r], xrecv.at[r], 1, to)
+            wait_bytes(xs.at[pl.ds(0, (hi - lo) * cap)], xsend.at[r])
+            if r == 0:
+                pl.semaphore_signal(pair_sem, inc=1, device_id=(0, peer(me, 1)), device_id_type=MESH)
+                pl.semaphore_wait(pair_sem, 1)
 
         @pl.loop(0, d_ff // WIDE)
         def _(j):
@@ -146,8 +134,7 @@
             dw1[:, cols] = jnp.zeros((d_model, WIDE), BF16)
 
         for c in range(n_col):
-            wait_bytes(dxr.at[c], dxrecv.at[c])
-            dx_ref[:, c * COL:(c + 1) * COL] = dot(perm[...], dxr[c], TN).astype(BF16)
+            wait_bytes(back.at[c], dxrecv.at[c])
         wait_bytes(ids_m, meta_sem.at[0])
         wait_bytes(gate_m, meta_sem.at[1])
 
@@ -190,7 +177,6 @@
 
         send_q(1)
         qr[place(0), :] = qs[block(me), :]
-        dx_ref[...] = jnp.zeros_like(dx_ref)
         for r, (lo, hi) in enumerate(CHUNKS):
             first = max(1, lo)
             wait_bytes(qr.at[pl.ds(first * cap, (hi - first) * cap)], qrecv.at[r])
@@ -207,23 +193,27 @@
                 da_ref[rows, cols] = (dh * b * sig * (1.0 + a * (1.0 - sig))).astype(BF16)
                 db_ref[rows, cols] = (dh * act).astype(BF16)
 
+            def dx_piece(c):
+                cols = pl.ds(pl.multiple_of(c * COL, COL), COL)
+                dxs[c, rows, :] = (dot(da_ref[rows, :], w1t[:, cols]) + dot(db_ref[rows, :], w3t[:, cols])).astype(BF16)
+                for k in range(lo, hi):
+                    send(dxs.at[c, place(k)], back.at[c, block(me)], dxsend, dxrecv.at[c], 0, peer(me, k))
+
+            pl.loop(0, n_col)(dx_piece)
+
             @pl.loop(0, n_col)
             def _(c):
                 cols = pl.ds(pl.multiple_of(c * COL, COL), COL)
-                dxs[c, rows, :] = (dot(da_ref[rows, :], w1t[:, cols]) + dot(db_ref[rows, :], w3t[:, cols])).astype(BF16)
-                for k in range(lo, hi):
-                    send(dxs.at[c, place(k)], dxr.at[c, block(me)], dxsend, dxrecv.at[c], 0, peer(me, k))
-
-            @pl.loop(0, n_col)
-            def _(c):
-                cols = pl.ds(pl.multiple_of(c * COL, COL), COL)
-                os[rows, cols] = dot(h_ref[rows, :], w2[:, cols]).astype(BF16)
+                os[c, rows, :] = dot(h_ref[rows, :], w2[:, cols]).astype(BF16)
 
             for k in range(lo, hi):
                 if k > 0:
-                    send(os.at[place(k)], yr.at[block(me)], osend, yrecv, 1, peer(me, k))
+                    for c in range(n_col):
+                        send(os.at[c, place(k)], back.at[c, block(me)], osend, yrecv, 1, peer(me, k))
             if r == 0:
-                yr[block(me), :] = os[place(0), :]
+                for c in range(n_col):
+                    back[c, block(me), :] = os[c, place(0), :]
+
         @pl.loop(0, d_ff // WIDE)
         def _(j):
             cols = pl.ds(pl.multiple_of(j * WIDE, WIDE), WIDE)
@@ -236,20 +226,31 @@
             dw1[:, cols] = dot(xt[...], da_ref[:, cols]).astype(BF16)
 
         others = pl.ds(0, n_rows - cap)
-        wait_bytes(yr.at[others], yrecv)
-        y_ref[...] = (gate_col * dot(perm[...], yr[...], TN)).astype(BF16)
+        wait_bytes(back.at[:, others], yrecv)
         wait_bytes(qs.at[others], qsend)
         wait_bytes(dxs, dxsend)
-        wait_bytes(os.at[others], osend)
-
-
-def store_kernel(xt, da_ref, db_ref, dw1_in, dw2_in, y_in, dx_in, dw1, dw3, dw2, y_out, dx_out, dw1_v, dw3_v, sem, piece_sem):
+        wait_bytes(os.at[:, others], osend)
+
+
+def store_kernel(
+    perm, gate, back, xt, da_ref, db_ref, dw1_in, dw2_in,
+    dw1, dw3, dw2, y_out, dx_out, dw1_v, dw3_v, tok_v, zero_v, sem, piece_sem,
+):
     stage = lax.axis_index("stage")
     d_ff = db_ref.shape[1]
-    pairs = ((dw2_in, dw2), (dw1_in, dw1.at[:, pl.ds(0, HERE)]), (y_in, y_out), (dx_in, dx_out))
+    pairs = ((dw2_in, dw2), (dw1_in, dw1.at[:, pl.ds(0, HERE)]))
     copies = [pltpu.make_async_copy(src, dst, sem.at[i]) for i, (src, dst) in enumerate(pairs)]
     for copy in copies:
         copy.start()
+
+    zero_v[...] = jnp.zeros_like(zero_v)
+
+    def put_tokens(held, empty):
+        tok_copies = [pltpu.make_async_copy(tok_v, held, sem.at[2]), pltpu.make_async_copy(zero_v, empty, sem.at[3])]
+        for copy in tok_copies:
+            copy.start()
+        for copy in tok_copies:
+            copy.wait()
 
     @pl.when(stage == 0)
     def _():
@@ -257,11 +258,17 @@
         zeros = [pltpu.make_async_copy(dw1_in.at[:, pl.ds(0, dst.shape[1])], dst, piece_sem.at[i]) for i, dst in enumerate(places)]
         for copy in zeros:
             copy.start()
+        for c in range(back.shape[0]):
+            tok_v[:, c * COL:(c + 1) * COL] = dot(perm[...], back[c], TN).astype(BF16)
+        put_tokens(dx_out, y_out)
         for copy in zeros:
             copy.wait()
 
     @pl.when(stage == 1)
     def _():
+        gate_col = gate_column(gate[...])
+        for c in range(back.shape[0]):
+            tok_v[:, c * COL:(c + 1) * COL] = (gate_col * dot(perm[...], back[c], TN)).astype(BF16)
         pieces = []
         for grad, held, out, skip in ((da_ref, dw1_v, dw1, HERE), (db_ref, dw3_v, dw3, 0)):
             for j in range((d_ff - skip) // PIECE):
@@ -270,6 +277,7 @@
                 held[:, here] = dot(xt[...], grad[:, there]).astype(BF16)
                 pieces.append(pltpu.make_async_copy(held.at[:, here], out.at[:, there], piece_sem.at[len(pieces)]))
                 pieces[-1].start()
+        put_tokens(y_out, dx_out)
         for piece in pieces:
             piece.wait()
 
@@ -296,22 +304,23 @@
         down = pltpu.VMEM((d_ff, d_model), BF16)
         tok = pltpu.VMEM((n_tok, d_model), BF16)
         dma = pltpu.SemaphoreType.DMA
-        y, dx, xt, da, db, dw1, dw2 = pl.pallas_call(
+        perm, gate, back, xt, da, db, dw1, dw2 = pl.pallas_call(
             functools.partial(exchange_kernel, n_group, cap),
-            out_shape=(tok, tok, pltpu.VMEM((d_model, n_rows), BF16), hidden, hidden, pltpu.VMEM((d_model, HERE), BF16), down),
+            out_shape=(
+                pltpu.VMEM((n_rows, n_tok), BF16), pltpu.VMEM((1, n_tok), F32), pieces,
+                pltpu.VMEM((d_model, n_rows), BF16), hidden, hidden, pltpu.VMEM((d_model, HERE), BF16), down,
+            ),
             in_specs=[hbm] * 7,
-            out_specs=(vmem,) * 7,
+            out_specs=(vmem,) * 8,
             scratch_shapes=[
                 up, up, down, down, down, up, blocks, blocks, hidden,
-                pltpu.VMEM((n_rows, n_tok), BF16),
-                blocks, blocks, pieces, pieces, blocks, blocks,
+                blocks, blocks, pieces, pieces,
                 pltpu.VMEM((1, n_tok), jnp.int32),
-                pltpu.VMEM((1, n_tok), F32),
                 tok,
                 dma((3,)),
                 dma((3,)),
                 dma((4,)),
-                dma((max(WINDOWS),)),
+                dma((len(CHUNKS),)),
                 dma((len(CHUNKS),)),
                 dma(()),
                 dma((len(CHUNKS),)),
@@ -319,6 +328,7 @@
                 dma((d_model // COL,)),
                 dma(()),
                 dma(()),
+                pltpu.SemaphoreType.REGULAR,
             ],
             compiler_params=pltpu.CompilerParams(
                 collective_id=0, has_side_effects=True, vmem_limit_bytes=48 * 2**20
@@ -328,7 +338,7 @@
             expert_ids.reshape(1, n_tok), gate_wts.reshape(1, n_tok), tokens_in[0], grad_out[0],
             w_gate[0, 0], w_up[0, 0], w_down[0, 0],
         )))
-        held = [pltpu.with_memory_space_constraint(v, pltpu.VMEM) for v in (xt, da, db, dw1, dw2, y, dx)]
+        held = [pltpu.with_memory_space_constraint(v, pltpu.VMEM) for v in (perm, gate, back, xt, da, db, dw1, dw2)]
         dw1, dw3, dw2, y, dx = pl.pallas_call(
             store_kernel,
             out_shape=(
@@ -338,9 +348,9 @@
                 jax.ShapeDtypeStruct((n_tok, d_model), BF16),
                 jax.ShapeDtypeStruct((n_tok, d_model), BF16),
             ),
-            in_specs=[vmem] * 7,
+            in_specs=[vmem] * 8,
             out_specs=(hbm,) * 5,
-            scratch_shapes=[pltpu.VMEM((d_model, d_ff - HERE), BF16), up, dma((4,)), dma(((2 * d_ff - HERE) // PIECE,))],
+            scratch_shapes=[pltpu.VMEM((d_model, d_ff - HERE), BF16), up, tok, tok, dma((4,)), dma(((2 * d_ff - HERE) // PIECE,))],
             compiler_params=pltpu.CompilerParams(vmem_limit_bytes=16 * 2**20),
             name="store",
         )(*held)

time: 41.4 us -> 40.8 us (0.986)
  Pallas kernels: 40.5 us -> 39.8 us
    pallas_call x1, Pallas kernels: 35.1 us -> 34.5 us  [device_fn(): pl.pallas_call(functools.partial(exchange_kernel, n_group, cap), out_shap...]
where the time goes in v5:
time: 40.8 us; the launch traced here: 40.7 us
  Pallas kernels  39.8 us (98%)
  between operations  0.8 us (2%)
    pallas_call x1, Pallas kernels, device_fn(): pl.pallas_call(functools.partial(exchange_kernel, n_group, cap), out_shap...  34.5 us
    pallas_call x1, Pallas kernels, device_fn(): pl.pallas_call(store_kernel, out_shape=(jax.ShapeDtypeStruct((d_model, d_...  5.39 us

profile of v5, /device:TPU:9, one launch (start us, length us, event | category | flops | bytes accessed | tf_op | source)
XLA Modules:
  0.0 40.7 jit_solution(10100699267953565580)
XLA Ops:
  0.6 34.5 %exchange.1 = (bf16[384,256]{1,0:T(8,128)(2,1)S(1)}, f32[1,256]{1,0:T(1,128)S(1)}, bf16[3,384,256]{2,1,0:T(8,128)(2,1)S(1)}, bf16[768,384]{1,0:T(8,128)(2,1)S(1)...) custom-call(s32[1,256]{1,0:T(1,128)} %bitcast.17, ...), custom_call_target="tpu_custom_call" | custom-call | tf_op jit(solution)/shard_map/exchange/pallas_call | solution.py:307
  35.1 5.4 %store.1 = (bf16[768,3072]{1,0:T(8,128)(2,1)}, bf16[768,3072]{1,0:T(8,128)(2,1)}, bf16[3072,768]{1,0:T(8,128)(2,1)}, bf16[256,768]{1,0:T(8,128)(2,1)}, bf16[256,768]{1,0:T(8,128)(2,1)}) custom-call(bf16[384,256]{1,0:T(8,128)(2,1)S(1)} %get-tuple-element.18.perm, f32[1,256]{1,0:T(1,128)S(1)} %get-tuple-element.19.gate, ...), custom_call_target="tpu_custom_call" | custom-call | tf_op jit(solution)/shard_map/store/pallas_call | solution.py:342

commit v6 on v5

--- a/solution.py
+++ b/solution.py
@@ -15,7 +15,7 @@
 TILE = 256
 CHUNKS = ((0, 4), (4, 8))
 HERE = 1536
-WIDE = 768
+WIDE = 1536
 NT = (((1,), (1,)), ((), ()))
 TN = (((0,), (0,)), ((), ()))
 PEERS = ((0, 0, 0), (0, 0, 1), (1, 1, 0), (1, 1, 1), (0, 1, 0), (0, 1, 1), (1, 0, 0), (1, 0, 1))
@@ -190,7 +190,7 @@
                 sig = jax.nn.sigmoid(a)
                 act = a * sig
                 h_ref[rows, cols] = (act * b).astype(BF16)
-                da_ref[rows, cols] = (dh * b * sig * (1.0 + a * (1.0 - sig))).astype(BF16)
+                da_ref[rows, cols] = (dh * b * (sig + act * (1.0 - sig))).astype(BF16)
                 db_ref[rows, cols] = (dh * act).astype(BF16)
 
             def dx_piece(c):

time: 40.8 us -> 40.4 us (level)
  no operation moved by 1% of the time
where the time goes in v6:
time: 40.4 us; the launch traced here: 40.3 us
  Pallas kernels  39.5 us (98%)
  between operations  0.82 us (2%)
    pallas_call x1, Pallas kernels, device_fn(): pl.pallas_call(functools.partial(exchange_kernel, n_group, cap), out_shap...  34.1 us
    pallas_call x1, Pallas kernels, device_fn(): pl.pallas_call(store_kernel, out_shape=(jax.ShapeDtypeStruct((d_model, d_...  5.39 us

profile of v6, /device:TPU:9, one launch (start us, length us, event | category | flops | bytes accessed | tf_op | source)
XLA Modules:
  0.0 40.3 jit_solution(719210467057509329)
XLA Ops:
  0.6 34.1 %exchange.1 = (bf16[384,256]{1,0:T(8,128)(2,1)S(1)}, f32[1,256]{1,0:T(1,128)S(1)}, bf16[3,384,256]{2,1,0:T(8,128)(2,1)S(1)}, bf16[768,384]{1,0:T(8,128)(2,1)S(1)...) custom-call(s32[1,256]{1,0:T(1,128)} %bitcast.17, ...), custom_call_target="tpu_custom_call" | custom-call | tf_op jit(solution)/shard_map/exchange/pallas_call | solution.py:307
  34.7 5.4 %store.1 = (bf16[768,3072]{1,0:T(8,128)(2,1)}, bf16[768,3072]{1,0:T(8,128)(2,1)}, bf16[3072,768]{1,0:T(8,128)(2,1)}, bf16[256,768]{1,0:T(8,128)(2,1)}, bf16[256,768]{1,0:T(8,128)(2,1)}) custom-call(bf16[384,256]{1,0:T(8,128)(2,1)S(1)} %get-tuple-element.18.perm, f32[1,256]{1,0:T(1,128)S(1)} %get-tuple-element.19.gate, ...), custom_call_target="tpu_custom_call" | custom-call | tf_op jit(solution)/shard_map/store/pallas_call | solution.py:342

commit v7 on v6

--- a/solution.py
+++ b/solution.py
@@ -205,11 +205,9 @@
             def _(c):
                 cols = pl.ds(pl.multiple_of(c * COL, COL), COL)
                 os[c, rows, :] = dot(h_ref[rows, :], w2[:, cols]).astype(BF16)
-
-            for k in range(lo, hi):
-                if k > 0:
-                    for c in range(n_col):
-                        send(os.at[c, place(k)], back.at[c, block(me)], osend, yrecv, 1, peer(me, k))
+                for k in range(max(1, lo), hi):
+                    send(os.at[c, place(k)], back.at[c, block(me)], osend, yrecv, 1, peer(me, k))
+
             if r == 0:
                 for c in range(n_col):
                     back[c, block(me), :] = os[c, place(0), :]

time: 40.4 us -> 40.4 us (level)
  no operation moved by 1% of the time
where the time goes in v7:
time: 40.4 us; the launch traced here: 40.3 us
  Pallas kernels  39.5 us (98%)
  between operations  0.82 us (2%)
    pallas_call x1, Pallas kernels, device_fn(): pl.pallas_call(functools.partial(exchange_kernel, n_group, cap), out_shap...  34.1 us
    pallas_call x1, Pallas kernels, device_fn(): pl.pallas_call(store_kernel, out_shape=(jax.ShapeDtypeStruct((d_model, d_...  5.39 us

profile of v7, /device:TPU:9, one launch (start us, length us, event | category | flops | bytes accessed | tf_op | source)
XLA Modules:
  0.0 40.3 jit_solution(2068320429801264503)
XLA Ops:
  0.6 34.1 %exchange.1 = (bf16[384,256]{1,0:T(8,128)(2,1)S(1)}, f32[1,256]{1,0:T(1,128)S(1)}, bf16[3,384,256]{2,1,0:T(8,128)(2,1)S(1)}, bf16[768,384]{1,0:T(8,128)(2,1)S(1)...) custom-call(s32[1,256]{1,0:T(1,128)} %bitcast.17, ...), custom_call_target="tpu_custom_call" | custom-call | tf_op jit(solution)/shard_map/exchange/pallas_call | solution.py:305
  34.7 5.4 %store.1 = (bf16[768,3072]{1,0:T(8,128)(2,1)}, bf16[768,3072]{1,0:T(8,128)(2,1)}, bf16[3072,768]{1,0:T(8,128)(2,1)}, bf16[256,768]{1,0:T(8,128)(2,1)}, bf16[256,768]{1,0:T(8,128)(2,1)}) custom-call(bf16[384,256]{1,0:T(8,128)(2,1)S(1)} %get-tuple-element.18.perm, f32[1,256]{1,0:T(1,128)S(1)} %get-tuple-element.19.gate, ...), custom_call_target="tpu_custom_call" | custom-call | tf_op jit(solution)/shard_map/store/pallas_call | solution.py:340
